TPU v7x, 256 devices: a whole 4x4x8 slice. The times are simulated.
256 devices in a mesh: tm: 32 (over y_lo, z, core), series: 8 (over x, y_hi).
Axes of the slice: x: 4, y: 4 (y_hi: 2, y_lo: 2; y = y_hi * 2 + y_lo), z: 8, core: 2. Of those that a mesh axis runs over, the one named last changes fastest.
Arguments:
- history: bfloat16 [16, 8192, 1024], P('series', 'tm'), may hold values from -36 to 36
- lengths: int32 [16], P('series'), may hold values from 512 to 8192
- head_window: int32 [16], replicated, may hold values from 32 to 512, as said below
- input_proj: bfloat16 [1024, 3072], replicated
- output_proj: bfloat16 [1024, 1024], replicated, may hold values from -0.1875 to 0.1875
- mixer_down: bfloat16 [1024, 512], replicated, may hold values from -0.1875 to 0.1875
- mixer_up: bfloat16 [512, 1024], replicated, may hold values from -0.25 to 0.25
- series_mix: bfloat16 [16, 16], replicated, may hold values from -1.5 to 1.5
Outputs:
- layer_out: bfloat16 [16, 8192, 1024], P('series', 'tm')
Inputs may be any that keep to these rules, and one draw needn't show every extreme that they name: `head_window`: some head has exactly 512.
All inputs are finite; a program needn't handle non-finite values.
Results may differ from a plain program's by a relative error of at most 0.0065.
Values may be sent and summed in bfloat16 or wider, within the bound.
A program may use at most 128 MiB of HBM per device.

v0:
```python
import jax
import jax.numpy as jnp
from jax import lax
from jax.sharding import PartitionSpec as P

HEADS = 16
WINDOW = 512


def from_behind(block, axis, distance):
    devices = range(lax.axis_size(axis))
    route = [(i - distance, i) for i in devices if i - distance in devices]
    return lax.ppermute(block, axis, route)


def attend_series(queries, keys_values, length, head_window, query_first, key_first, patches):
    query_rows = queries.shape[0]
    model_width = queries.shape[1]
    key_rows = keys_values.shape[0]
    head_size = model_width // HEADS
    group_heads = min(4, HEADS)
    group_count = HEADS // group_heads
    group_width = group_heads * head_size
    query_pos = query_first + jnp.arange(query_rows, dtype=jnp.int32)
    key_pos = key_first + jnp.arange(key_rows, dtype=jnp.int32)
    key_valid = (key_pos >= patches - length) & (key_pos < patches)
    distance = jnp.abs(query_pos[:, None] - key_pos[None, :])

    def per_group(group_index):
        column = group_index * group_width
        group_queries = lax.dynamic_slice_in_dim(queries, column, group_width, 1).reshape(
            query_rows, group_heads, head_size
        )
        group_keys = lax.dynamic_slice_in_dim(keys_values, column, group_width, 1).reshape(
            key_rows, group_heads, head_size
        )
        group_values = lax.dynamic_slice_in_dim(
            keys_values, model_width + column, group_width, 1
        ).reshape(key_rows, group_heads, head_size)
        reaches = lax.dynamic_slice_in_dim(head_window, group_index * group_heads, group_heads, 0)
        scores = jnp.einsum(
            "qhd,khd->hqk", group_queries, group_keys, preferred_element_type=jnp.float32
        ) * head_size ** (-0.5)
        allowed = (distance[None, :, :] <= reaches[:, None, None]) & key_valid[None, None, :]
        scores = jnp.where(allowed, scores, -1e30)
        largest = jnp.max(scores, axis=-1, keepdims=True)
        weights = jnp.exp(scores - largest)
        totals = jnp.sum(weights, axis=-1)
        probabilities = weights.astype(jnp.bfloat16)
        combined = (
            jnp.einsum(
                "hqk,khd->qhd", probabilities, group_values, preferred_element_type=jnp.float32
            )
            / jnp.transpose(totals)[:, :, None]
        )
        return combined.reshape(query_rows, group_width)

    grouped = lax.map(per_group, jnp.arange(group_count, dtype=jnp.int32))
    combined = jnp.transpose(grouped, (1, 0, 2)).reshape(query_rows, model_width)
    query_valid = query_pos >= patches - length
    return jnp.where(query_valid[:, None], combined, 0.0).astype(jnp.bfloat16)


def on_device(
    history, lengths, head_window, input_proj, output_proj, mixer_down, mixer_up, series_mix
):
    local_series, local_patches, model_width = history.shape
    packed = jnp.einsum(
        "spd,de->spe", history, input_proj, preferred_element_type=jnp.float32
    ).astype(jnp.bfloat16)
    queries = packed[:, :, :model_width]
    keys_values = packed[:, :, model_width:]
    hops_count = -(-WINDOW // local_patches)
    earlier = []
    following = []
    kv_weight = input_proj[:, model_width:]
    for offset in range(1, hops_count + 1):
        before_rows = from_behind(history, "tm", offset)
        after_rows = from_behind(history, "tm", -offset)
        earlier.insert(
            0,
            jnp.einsum(
                "spd,de->spe", before_rows, kv_weight, preferred_element_type=jnp.float32
            ).astype(jnp.bfloat16),
        )
        following.append(
            jnp.einsum(
                "spd,de->spe", after_rows, kv_weight, preferred_element_type=jnp.float32
            ).astype(jnp.bfloat16)
        )
    context = jnp.concatenate(earlier + [keys_values] + following, axis=1)
    position = lax.axis_index("tm")
    patches = local_patches * lax.axis_size("tm")
    query_first = position * local_patches
    key_first = (position - hops_count) * local_patches

    def per_series(inputs):
        series_queries, series_context, length = inputs
        return attend_series(
            series_queries, series_context, length, head_window, query_first, key_first, patches
        )

    attended = lax.map(per_series, (queries, context, lengths))
    hidden = (
        history.astype(jnp.float32)
        + jnp.einsum("spd,de->spe", attended, output_proj, preferred_element_type=jnp.float32)
    ).astype(jnp.bfloat16)
    branch = jnp.einsum(
        "spd,dc->spc", hidden, mixer_down, preferred_element_type=jnp.float32
    ).astype(jnp.bfloat16)
    series_first = lax.axis_index("series") * local_series
    own_rows = lax.dynamic_slice_in_dim(series_mix, series_first, local_series, 0)
    combined = jnp.einsum(
        "ab,bpc->apc",
        own_rows,
        lax.all_gather(branch, "series", axis=0, tiled=True),
        preferred_element_type=jnp.float32,
    )
    combined = combined.astype(jnp.bfloat16)
    update = jnp.einsum("spc,cd->spd", combined, mixer_up, preferred_element_type=jnp.float32)
    return (hidden.astype(jnp.float32) + update).astype(jnp.bfloat16)


def solution(mesh):
    in_specs = (P("series", "tm", None), P("series"), P(), P(), P(), P(), P(), P())
    out_specs = P("series", "tm", None)
    return jax.shard_map(
        on_device, mesh=mesh, in_specs=in_specs, out_specs=out_specs, check_vma=False
    )
```

profile of v0, /device:TPU:9, one launch (start us, length us, event | category | flops | bytes accessed | tf_op | source)
XLA Modules:
  0.0 278.6 jit_solution(16059605942084409501)
XLA Ops:
  6.5 3.7 %collective-permute-start = (bf16[2,256,1024]{2,1,0:T(8,128)(2,1)}, bf16[2,256,1024]{2,1,0:T(8,128)(2,1)}, u32[]{:S(2)}, u32[]{:S(2)}) collective-permute-start(bf16[2,256,1024]{2,1,0:T(8,128)(2,1)} %param.12), channel_id=1, source_target_pairs={{0,16},{8,24},{16,32},{24,40},{32,48},{40,56},{48,64},{56,72},{64,... | collective-permute-start | bytes 3145736 | tf_op jit(solution)/shard_map/ppermute | solution.py:13
  10.2 4.4 %collective-permute-start.1 = (bf16[2,256,1024]{2,1,0:T(8,128)(2,1)}, bf16[2,256,1024]{2,1,0:T(8,128)(2,1)}, u32[]{:S(2)}, u32[]{:S(2)}) collective-permute-start(bf16[2,256,1024]{2,1,0:T(8,128)(2,1)} %param.12), channel_id=1, source_target_pairs={{0,8},{8,16},{16,24},{24,32},{32,40},{40,48},{48,56},{56,64},{64,7... | collective-permute-start | bytes 3145736 | tf_op jit(solution)/shard_map/ppermute | solution.py:13
  14.6 1.9 collective-permute-start.2
  16.5 3.9 %collective-permute-start.3 = (bf16[2,256,1024]{2,1,0:T(8,128)(2,1)}, bf16[2,256,1024]{2,1,0:T(8,128)(2,1)S(1)}, u32[]{:S(2)}, u32[]{:S(2)}) collective-permute-start(bf16[2,256,1024]{2,1,0:T(8,128)(2,1)} %param.12), channel_id=1, source_target_pairs={{16,0},{24,8},{32,16},{40,24},{48,32},{56,40},{64,48},{72,56},{80,... | collective-permute-start | bytes 3145736 | tf_op jit(solution)/shard_map/ppermute | solution.py:13
  20.5 6.5 %fusion.22 = bf16[2,256,3072]{2,1,0:T(8,128)(2,1)S(1)} fusion(bf16[2,256,1024]{2,1,0:T(8,128)(2,1)} %param.12, bf16[1024,3072]{1,0:T(8,128)(2,1)} %param.15), kind=kOutput, calls=%fused_computation.29 | convolution fusion | flops 3222798336 | bytes 10485760 | tf_op jit(solution)/shard_map/spd,de->spe/dot_general | solution.py:68
  27.1 1.6 copy-done.2
  29.8 7.4 %collective-permute-done = bf16[2,256,1024]{2,1,0:T(8,128)(2,1)} collective-permute-done((bf16[2,256,1024]{2,1,0:T(8,128)(2,1)}, bf16[2,256,1024]{2,1,0:T(8,128)(2,1)}, u32[]{:S(2)}, u32[]{:S(2)}) %collective-permute-start) | collective-permute-done | bytes 1048608 | tf_op jit(solution)/shard_map/ppermute | solution.py:13
  37.2 5.0 %fusion.38 = bf16[2,1280,2048]{2,1,0:T(8,128)(2,1)S(1)} fusion(bf16[2,256,1024]{2,1,0:T(8,128)(2,1)} %collective-permute-done, bf16[1024,3072]{1,0:T(8,128)(2,1)} %param.15), kind=kOutput, calls=%fused_computation.41 | convolution fusion | flops 2148532224 | bytes 7340032 | tf_op jit(solution)/shard_map/spd,de->spe/dot_general | solution.py:82
  42.2 2.5 collective-permute-done.1
  44.7 4.8 %fusion.44 = bf16[2,1280,2048]{2,1,0:T(8,128)(2,1)S(1)} fusion(bf16[2,1280,2048]{2,1,0:T(8,128)(2,1)S(1)} %fusion.38, bf16[2,256,1024]{2,1,0:T(8,128)(2,1)} %collective-permute-done.1, bf16[1024,3072]{1,0:T(8,128)(2,1)} %param.15), kind=kOutput, calls=%fused_computation.43 | convolution fusion | flops 2148532224 | bytes 7340032 | tf_op jit(solution)/shard_map/spd,de->spe/dot_general | solution.py:82
  49.8 3.6 %fusion.50 = bf16[2,1280,2048]{2,1,0:T(8,128)(2,1)S(1)} fusion(bf16[2,1280,2048]{2,1,0:T(8,128)(2,1)S(1)} %slice_dynamic-update-slice_fusion, bf16[2,256,1024]{2,1,0:T(8,128)(2,1)} %collective-permute-done.2, bf16[1024,3072]{1,0:T(8,128)(2,1)S(1)} %bitcast.116), kind=kOutput, calls=%fused_computation.45 | convolution fusion | flops 2148532224 | bytes 7340032 | tf_op jit(solution)/shard_map/spd,de->spe/dot_general | solution.py:87
  53.4 2.3 fusion.56
  55.8 4.0 %copy-done.1 = bf16[2,1280,2048]{2,1,0:T(8,128)(2,1)} copy-done((bf16[2,1280,2048]{2,1,0:T(8,128)(2,1)}, bf16[2,1280,2048]{2,1,0:T(8,128)(2,1)S(1)}, u32[]{:S(2)}) %copy-start.1) | copy-done | bytes 10485784
  59.7 119.3 %while.33 = (s32[]{:T(128)}, bf16[2,256,1024]{1,2,0:T(8,128)(2,1)}, s32[]{:T(128)}, s32[2]{0:T(128)S(1)}, bf16[2,256,1024]{2,1,0:T(8,128)(2,1)}, /*index=5*/bf16...) while((s32[]{:T(128)}, bf16[2,256,1024]{1,2,0:T(8,128)(2,1)}, ...), condition=%wide.region_5.6_spmd, body=%wide.region_0.5_spmd.sunk | while | flops 348394496 | bytes 47223572 | solution.py:103
  61.1 5.6 %constant_dynamic-slice_fusion.9 = bf16[1,1280,2048]{2,1,0:T(8,128)(2,1)} fusion(bf16[2,1280,2048]{2,1,0:T(8,128)(2,1)} %get-tuple-element.545, s32[]{:T(128)} %get-tuple-element.521), kind=kLoop, calls=%fused_computation.25.clone.1 | loop fusion | bytes 10485764 | tf_op jit(solution)/shard_map/while/body/jit(dynamic_index_in_dim)/dynamic_slice | solution.py:103
  66.7 7.9 %copy.26 = bf16[1,1280,2048]{1,2,0:T(8,128)(2,1)} copy(bf16[1,1280,2048]{2,1,0:T(8,128)(2,1)} %constant_dynamic-slice_fusion.9) | data formatting | bytes 10485760 | tf_op jit(solution)/shard_map/while/body/jit(dynamic_index_in_dim)/dynamic_slice | solution.py:103
  77.3 40.2 %while.34 = (s32[]{:T(128)}, bf16[4,256,256]{1,2,0:T(8,128)(2,1)}, s32[4]{0:T(128)}, bf16[1280,2048]{0,1:T(8,128)(2,1)}, s32[16]{0:T(128)}, /*index=5*/bf16[256,...) while((s32[]{:T(128)}, bf16[4,256,256]{1,2,0:T(8,128)(2,1)}, ...), condition=%wide.region_4.4_spmd.clone, body=%wide.region_1.3_spmd.clone.sunk | while | flops 348130304 | bytes 23098768 | solution.py:58
  77.3 1.2 dynamic_slice.82
  79.1 1.4 constant_dynamic-slice_fusion.11
  82.9 1.8 fusion.98
  87.4 1.2 dynamic_slice.82
  89.1 1.4 constant_dynamic-slice_fusion.11
  93.0 1.8 fusion.98
  97.4 1.2 dynamic_slice.82
  99.2 1.4 constant_dynamic-slice_fusion.11
  103.0 1.8 fusion.98
  107.4 1.2 dynamic_slice.82
  109.2 1.4 constant_dynamic-slice_fusion.11
  113.1 1.8 fusion.98
  117.5 1.9 fusion.92
  120.8 5.6 %constant_dynamic-slice_fusion.9 = bf16[1,1280,2048]{2,1,0:T(8,128)(2,1)} fusion(bf16[2,1280,2048]{2,1,0:T(8,128)(2,1)} %get-tuple-element.545, s32[]{:T(128)} %get-tuple-element.521), kind=kLoop, calls=%fused_computation.25.clone.1 | loop fusion | bytes 10485764 | tf_op jit(solution)/shard_map/while/body/jit(dynamic_index_in_dim)/dynamic_slice | solution.py:103
  126.4 7.9 %copy.26 = bf16[1,1280,2048]{1,2,0:T(8,128)(2,1)} copy(bf16[1,1280,2048]{2,1,0:T(8,128)(2,1)} %constant_dynamic-slice_fusion.9) | data formatting | bytes 10485760 | tf_op jit(solution)/shard_map/while/body/jit(dynamic_index_in_dim)/dynamic_slice | solution.py:103
  137.0 40.2 %while.34 = (s32[]{:T(128)}, bf16[4,256,256]{1,2,0:T(8,128)(2,1)}, s32[4]{0:T(128)}, bf16[1280,2048]{0,1:T(8,128)(2,1)}, s32[16]{0:T(128)}, /*index=5*/bf16[256,...) while((s32[]{:T(128)}, bf16[4,256,256]{1,2,0:T(8,128)(2,1)}, ...), condition=%wide.region_4.4_spmd.clone, body=%wide.region_1.3_spmd.clone.sunk | while | flops 348130304 | bytes 23098768 | solution.py:58
  137.0 1.2 dynamic_slice.82
  138.8 1.4 constant_dynamic-slice_fusion.11
  142.6 1.8 fusion.98
  148.8 1.4 constant_dynamic-slice_fusion.11
  152.7 1.8 fusion.98
  158.9 1.4 constant_dynamic-slice_fusion.11
  162.7 1.8 fusion.98
  168.9 1.4 constant_dynamic-slice_fusion.11
  172.7 1.8 fusion.98
  177.2 1.9 fusion.92
  179.1 2.9 %add_convert_fusion.1 = bf16[2,256,1024]{2,1,0:T(8,128)(2,1)S(1)} fusion(bf16[2,256,1024]{2,1,0:T(8,128)(2,1)} %param.12, bf16[2,256,1024]{1,2,0:T(8,128)(2,1)} %get-tuple-element.223, bf16[1024,1024]{1,0:T(8,128)(2,1)S(1)} %copy-done), kind=kOutput, calls=%fused_computation.56 | convolution fusion | flops 1075314688 | bytes 5242880 | tf_op jit(solution)/shard_map/spd,de->spe/dot_general | solution.py:106
  183.0 1.5 convolution_convert_fusion
  184.5 79.6 %all-gather.2.cloned.1.call-done = bf16[16,256,512]{2,1,0:T(8,128)(2,1)} async-done(((bf16[2,256,512]{2,1,0:T(8,128)(2,1)}), bf16[16,256,512]{2,1,0:T(8,128)(2,1)}) %all-gather.2.cloned.1.call-update) | async-done | bytes 4194320 | tf_op jit(solution)/shard_map/all_gather | solution.py:116
  264.1 4.8 %fusion.33 = bf16[2,256,512]{2,0,1:T(2,128)(2,1)S(1)} fusion(bf16[16,256,512]{2,1,0:T(8,128)(2,1)} %all-gather.2.cloned.1.call-done, bf16[16,16]{1,0:T(8,128)(2,1)} %param.19, s32[]{:T(128)S(6)} %select_n.48), kind=kOutput, calls=%fused_computation.38 | convolution fusion | flops 8388608 | bytes 4719108 | tf_op jit(solution)/shard_map/ab,bpc->apc/dot_general | solution.py:113
  268.9 2.9 %add_convert_fusion = bf16[2,256,1024]{2,1,0:T(8,128)(2,1)} fusion(bf16[2,256,1024]{2,1,0:T(8,128)(2,1)} %copy-done.7, bf16[512,1024]{1,0:T(8,128)(2,1)S(1)} %copy-done.5, bf16[2,256,512]{2,0,1:T(2,128)(2,1)S(1)} %fusion.33), kind=kOutput, calls=%fused_computation.55 | convolution fusion | flops 538443776 | bytes 3670016 | tf_op jit(solution)/shard_map/spc,cd->spd/dot_general | solution.py:120
  (101 shorter events, 48.8 us)
Async XLA Ops:
  6.5 172.6 %copy-start = (bf16[1024,1024]{1,0:T(8,128)(2,1)S(1)}, bf16[1024,1024]{1,0:T(8,128)(2,1)}, u32[]{:S(2)}) copy-start(bf16[1024,1024]{1,0:T(8,128)(2,1)} %param.16) | copy-start | bytes 6291460
  6.5 257.6 %all-gather.2.cloned.1.call-start = ((), (), s32[]{:S(2)}) async-start(), calls=%async_computation | async-start | bytes 4718592 | tf_op jit(solution)/shard_map/all_gather | solution.py:116
  6.5 30.7 %collective-permute-start = (bf16[2,256,1024]{2,1,0:T(8,128)(2,1)}, bf16[2,256,1024]{2,1,0:T(8,128)(2,1)}, u32[]{:S(2)}, u32[]{:S(2)}) collective-permute-start(bf16[2,256,1024]{2,1,0:T(8,128)(2,1)} %param.12), channel_id=1, source_target_pairs={{0,16},{8,24},{16,32},{24,40},{32,48},{40,56},{48,64},{56,72},{64,... | collective-permute-start | bytes 3145736 | tf_op jit(solution)/shard_map/ppermute | solution.py:13
  10.2 34.5 %collective-permute-start.1 = (bf16[2,256,1024]{2,1,0:T(8,128)(2,1)}, bf16[2,256,1024]{2,1,0:T(8,128)(2,1)}, u32[]{:S(2)}, u32[]{:S(2)}) collective-permute-start(bf16[2,256,1024]{2,1,0:T(8,128)(2,1)} %param.12), channel_id=1, source_target_pairs={{0,8},{8,16},{16,24},{24,32},{32,40},{40,48},{48,56},{56,64},{64,7... | collective-permute-start | bytes 3145736 | tf_op jit(solution)/shard_map/ppermute | solution.py:13
  14.6 35.2 %collective-permute-start.2 = (bf16[2,256,1024]{2,1,0:T(8,128)(2,1)}, bf16[2,256,1024]{2,1,0:T(8,128)(2,1)}, u32[]{:S(2)}, u32[]{:S(2)}) collective-permute-start(bf16[2,256,1024]{2,1,0:T(8,128)(2,1)} %param.12), channel_id=1, source_target_pairs={{8,0},{16,8},{24,16},{32,24},{40,32},{48,40},{56,48},{64,56},{72,6... | collective-permute-start | bytes 3145736 | tf_op jit(solution)/shard_map/ppermute | solution.py:13
  16.5 36.9 %collective-permute-start.3 = (bf16[2,256,1024]{2,1,0:T(8,128)(2,1)}, bf16[2,256,1024]{2,1,0:T(8,128)(2,1)S(1)}, u32[]{:S(2)}, u32[]{:S(2)}) collective-permute-start(bf16[2,256,1024]{2,1,0:T(8,128)(2,1)} %param.12), channel_id=1, source_target_pairs={{16,0},{24,8},{32,16},{40,24},{48,32},{56,40},{64,48},{72,56},{80,... | collective-permute-start | bytes 3145736 | tf_op jit(solution)/shard_map/ppermute | solution.py:13
  27.1 1.7 copy-start.2
  37.2 12.6 %slice-start = ((s8[6291456]{0:T(1024)(128)(4,1)}), s8[4194304]{0:T(1024)(128)(4,1)S(1)}, s32[]{:S(2)}) async-start(s8[6291456]{0:T(1024)(128)(4,1)} %bitcast.115), calls=%async_computation.1 | async-start | bytes 8388608
  42.2 7.4 %copy-start.3 = (bf16[2,256,3072]{2,1,0:T(8,128)(2,1)S(1)}, bf16[2,256,3072]{2,1,0:T(8,128)(2,1)}, u32[]{:S(2)}) copy-start(bf16[2,256,3072]{2,1,0:T(8,128)(2,1)} %copy-done.2) | copy-start | bytes 9437188
  42.2 7.6 %slice-start.1 = ((s8[6291456]{0:T(1024)(128)(4,1)}), s8[2097152]{0:T(1024)(128)(4,1)S(1)}, s32[]{:S(2)}) async-start(s8[6291456]{0:T(1024)(128)(4,1)} %bitcast.115), calls=%async_computation.2 | async-start | bytes 4194304
  53.4 6.4 %copy-start.6 = (s32[2]{0:T(128)S(1)}, s32[2]{0:T(128)}, u32[]{:S(2)}) copy-start(s32[2]{0:T(128)} %param.13) | copy-start | bytes 28
  55.7 4.0 %copy-start.1 = (bf16[2,1280,2048]{2,1,0:T(8,128)(2,1)}, bf16[2,1280,2048]{2,1,0:T(8,128)(2,1)S(1)}, u32[]{:S(2)}) copy-start(bf16[2,1280,2048]{2,1,0:T(8,128)(2,1)S(1)} %fusion.56) | copy-start | bytes 31457284
  179.1 3.9 %copy-start.4 = (bf16[1024,512]{1,0:T(8,128)(2,1)S(1)}, bf16[1024,512]{1,0:T(8,128)(2,1)}, u32[]{:S(2)}) copy-start(bf16[1024,512]{1,0:T(8,128)(2,1)} %param.17) | copy-start | bytes 3145732
  182.0 1.0 copy-start.7
  183.0 85.9 %copy-start.5 = (bf16[512,1024]{1,0:T(8,128)(2,1)S(1)}, bf16[512,1024]{1,0:T(8,128)(2,1)}, u32[]{:S(2)}) copy-start(bf16[512,1024]{1,0:T(8,128)(2,1)} %param.18) | copy-start | bytes 3145732
Sparse Core Ops, SparseCore 0:
  184.6 79.4 all-gather.1
where the time goes:
time: 282 us; the launch traced here: 279 us
  waiting for transfers between devices  89.6 us (32%)
  local copies, waits for them, and re-layouts  80.8 us (29%)
  matrix products  56.5 us (20%)
  starting transfers between devices  13.9 us (5%)
  other arithmetic  13.6 us (5%)
  between operations  13.6 us (5%)
  loops' own time  10.6 us (4%)
    all_gather x1, waiting for transfers between devices, on_device(): lax.all_gather(branch, 'series', axis=0, tiled=True)  79.6 us
    dynamic_slice x10, local copies, waits for them, and re-layouts, on_device(): attended = lax.map(per_series, (queries, context, lengths))  32.6 us
    dot_general x8, matrix products, per_group(): jnp.einsum('qhd,khd->hqk', group_queries, group_keys, preferred_element_t...  14.2 us
    ppermute x4, starting transfers between devices, from_behind(): return lax.ppermute(block, axis, route)  13.9 us
    dynamic_slice x8, local copies, waits for them, and re-layouts, per_group(): lax.dynamic_slice_in_dim(keys_values, column, group_width, 1)  11 us
    ppermute x4, waiting for transfers between devices, from_behind(): return lax.ppermute(block, axis, route)  9.95 us
    dot_general x2, matrix products, on_device(): jnp.einsum('spd,de->spe', before_rows, kv_weight, preferred_element_type=...  9.83 us
    dynamic_slice x8, local copies, waits for them, and re-layouts, attend_series(): grouped = lax.map(per_group, jnp.arange(group_count, dtype=jnp.int32))  9.73 us
  transfers between devices with their start and end apart: 5, of which 3 were waited for; matrix products, arithmetic and copies ran while one was open for 8% of the time, Pallas kernels for 0%

commit v1 on v0

v1 whole, which is shorter than its diff:
```python
import functools
import math

import jax
import jax.numpy as jnp
from jax import lax
from jax.experimental import pallas as pl
from jax.experimental.pallas import tpu as pltpu
from jax.sharding import PartitionSpec as P

HEAD_SIZE = 64
PAIR = 2 * HEAD_SIZE
NEG = -1e30
FAR = 1 << 20
MESH = pl.DeviceIdType.MESH
BF16 = jnp.bfloat16
F32 = jnp.float32
SCALE = HEAD_SIZE ** -0.5 * math.log2(math.e)


def nt_dot(a, b):
    return lax.dot_general(a, b, (((1,), (1,)), ((), ())), preferred_element_type=F32)


def nn_dot(a, b):
    return jnp.dot(a, b, preferred_element_type=F32)


def layer_kernel(
    dims, lengths, window, mix, hist, wi_any, wo_any, wd_any, wu_any, out,
    X, Q, K, VO, M, L, ACC, DIST, ATT, HID, BR, RX, KR, CB, CI, HS, wi, wo, wd, wu,
    loc_sem, sib_sem, hs_sem, rs_sem, rr_sem, a1s, a1r, a2s, a2r,
):
    chips, groups = dims
    members = 2 * groups
    _, R, D = hist.shape
    B = 2 * R
    RC = R // 2
    C = BR.shape[1]
    CH = B // members
    pairs = D // PAIR
    me = lax.axis_index("tm")
    g = lax.axis_index("series")
    c = lax.rem(me, 2)
    chip = me // 2
    other = 1 - c
    sib = chip * 2 + other
    mine = g * 2 + c
    rchip = lax.rem(chip + 1, chips)
    lchip = lax.rem(chip + chips - 1, chips)
    total = chips * B

    def member(j):
        p = lax.rem(mine + j, members)
        return p, p // 2, lax.rem(p, 2)

    barrier = pltpu.get_barrier_semaphore()
    for nchip in (lchip, rchip):
        for core in range(2):
            pl.semaphore_signal(
                barrier, inc=1, device_id={"tm": nchip * 2 + core}, device_id_type=MESH
            )
    for j in range(1, members):
        _, pg, pc = member(j)
        pl.semaphore_signal(
            barrier, inc=1, device_id={"tm": chip * 2 + pc, "series": pg}, device_id_type=MESH
        )
    own_rows = pl.multiple_of(B + c * R, R)
    own_load = pltpu.make_async_copy(hist.at[c], X.at[pl.ds(own_rows, R)], loc_sem.at[0])
    own_load.start()
    loads = [
        pltpu.make_async_copy(src, dst, loc_sem.at[1 + i])
        for i, (src, dst) in enumerate(((wi_any, wi), (wo_any, wo), (wd_any, wd), (wu_any, wu)))
    ]
    for load in loads:
        load.start()
    pl.semaphore_wait(barrier, 4 + members - 1)

    sib_copy = pltpu.make_async_remote_copy(
        src_ref=hist.at[other], dst_ref=X.at[pl.ds(own_rows, R)],
        send_sem=sib_sem.at[0], recv_sem=sib_sem.at[1],
        device_id={"tm": sib}, device_id_type=MESH,
    )
    sib_copy.start()

    def halo_copy(phase, k, s):
        if phase == 0:
            target = jnp.where(c == 1, rchip, lchip)
            side = 1 - c
            kk = k + c * (1 - 2 * k)
            base = 2 * B + c * (R - 2 * B)
        else:
            target = jnp.where(c == 1, lchip, rchip)
            side = c
            kk = (1 - k) + c * (2 * k - 1)
            base = c * (2 * B + R)
        row = pl.multiple_of(base + kk * RC, RC)
        return pltpu.make_async_remote_copy(
            src_ref=hist.at[s, pl.ds(pl.multiple_of(kk * RC, RC), RC)],
            dst_ref=X.at[pl.ds(row, RC)],
            send_sem=rs_sem.at[phase, k, s], recv_sem=rr_sem.at[phase, side, k],
            device_id={"tm": target * 2 + s}, device_id_type=MESH,
        )

    def halo_arrived(phase, side, k):
        near_first = (1 - k) if side == 0 else k
        base = ((R, 2 * B), (0, 2 * B + R))[phase][side]
        pltpu.make_async_remote_copy(
            src_ref=hist.at[0, pl.ds(0, RC)],
            dst_ref=X.at[pl.ds(base + near_first * RC, RC)],
            send_sem=rs_sem.at[phase, k, 0], recv_sem=rr_sem.at[phase, side, k],
            device_id={"tm": sib}, device_id_type=MESH,
        ).wait_recv()

    near = [halo_copy(0, k, s) for k in range(2) for s in range(2)]
    far = [halo_copy(1, k, s) for k in range(2) for s in range(2)]
    for copy in near:
        copy.start()

    for p in range(pairs):
        VO[:, p * 2 * PAIR + PAIR:(p + 1) * 2 * PAIR] = jnp.ones((3 * B, PAIR), BF16)

    tile = 256

    def project(first, count, with_queries):
        rows = pl.ds(first, count)

        if with_queries:
            @pl.loop(0, D // tile)
            def _(j):
                cols = pl.ds(pl.multiple_of(j * tile, tile), tile)
                Q[:, cols] = (nn_dot(X[rows, :], wi[:, cols]) * SCALE).astype(BF16)

        @pl.loop(0, D // tile)
        def _(j):
            cols = pl.ds(pl.multiple_of(j * tile, tile), tile)
            wcols = pl.ds(pl.multiple_of(D + j * tile, tile), tile)
            K[rows, cols] = nn_dot(X[rows, :], wi[:, wcols]).astype(BF16)

        @pl.loop(0, D // tile)
        def _(j):
            wcols = pl.ds(pl.multiple_of(2 * D + j * tile, tile), tile)
            values = nn_dot(X[rows, :], wi[:, wcols]).astype(BF16)
            for i in range(tile // PAIR):
                at = pl.multiple_of((j * (tile // PAIR) + i) * 2 * PAIR, 2 * PAIR)
                VO[rows, pl.ds(at, PAIR)] = values[:, i * PAIR:(i + 1) * PAIR]

    length = lengths[c]
    first_valid = total - length

    def distances(q_first, q_count, k_ranges, at):
        column = 0
        for k_first, k_count in k_ranges:
            qi = q_first + lax.broadcasted_iota(jnp.int32, (q_count, k_count), 0)
            kj = k_first + lax.broadcasted_iota(jnp.int32, (q_count, k_count), 1)
            kpos = chip * B + kj
            valid = (kpos >= first_valid) & (kpos < total) & (kpos >= 0)
            DIST[at:at + q_count, column:column + k_count] = jnp.where(
                valid, jnp.abs(qi - kj), FAR
            )
            column += k_count

    lane = lax.broadcasted_iota(jnp.int32, (R, PAIR), 1)
    low = lane < HEAD_SIZE

    def attend(q_first, k_ranges, at, hp, first, last):
        q_rows = slice(q_first, q_first + R)
        cols = pl.ds(pl.multiple_of(hp * PAIR, PAIR), PAIR)
        vcols = pl.ds(pl.multiple_of(hp * 2 * PAIR, 2 * PAIR), 2 * PAIR)
        q = Q[q_rows, cols]
        zero = jnp.zeros_like(q)
        both = jnp.concatenate([jnp.where(low, q, zero), jnp.where(low, zero, q)], axis=0)
        pieces = []
        column = 0
        for k_first, k_count in k_ranges:
            keys = K[B + k_first:B + k_first + k_count, cols]
            s = nt_dot(both, keys)
            dist = DIST[at:at + R, column:column + k_count]
            pieces.append((
                jnp.where(dist <= window[2 * hp], s[:R], NEG),
                jnp.where(dist <= window[2 * hp + 1], s[R:], NEG),
            ))
            column += k_count
        tops = []
        for h in range(2):
            top = functools.reduce(
                jnp.maximum, [jnp.max(piece[h], axis=1, keepdims=True) for piece in pieces]
            )
            tops.append(top)
        if not first:
            old = M[q_rows, cols]
            tops = [
                jnp.maximum(tops[0], old[:, 0:1]),
                jnp.maximum(tops[1], old[:, HEAD_SIZE:HEAD_SIZE + 1]),
            ]
        new = jnp.where(low, tops[0], tops[1])
        added = None
        for (k_first, k_count), piece in zip(k_ranges, pieces):
            p = jnp.concatenate(
                [jnp.exp2(piece[0] - tops[0]), jnp.exp2(piece[1] - tops[1])], axis=0
            ).astype(BF16)
            part = nn_dot(p, VO[B + k_first:B + k_first + k_count, vcols])
            added = part if added is None else added + part
        acc = jnp.where(low, added[:R, :PAIR], added[R:, :PAIR])
        sums = jnp.where(low, added[:R, PAIR:], added[R:, PAIR:])
        if not first:
            alpha = jnp.exp2(old - new)
            acc = acc + ACC[q_rows, cols] * alpha
            sums = sums + L[q_rows, cols] * alpha
        if last:
            qpos = chip * B + q_first + lax.broadcasted_iota(jnp.int32, (R, PAIR), 0)
            ATT[q_rows, cols] = jnp.where(qpos >= first_valid, acc / sums, 0.0).astype(BF16)
        else:
            M[q_rows, cols] = new
            ACC[q_rows, cols] = acc
            L[q_rows, cols] = sums

    own_load.wait()
    sib_copy.wait_recv()
    loads[0].wait()
    project(B, B, True)
    own_keys = ((0, B),)
    distances(0, B, own_keys, 0)

    def own_stage(hp):
        for b in range(2):
            attend(b * R, own_keys, b * R, hp, True, False)

    pl.loop(0, pairs // 2)(own_stage)
    for copy in near:
        copy.wait_send()
    for copy in far:
        copy.start()
    pl.loop(pairs // 2, pairs)(own_stage)

    for k in range(2):
        for side in range(2):
            halo_arrived(0, side, k)
    project(R, R, False)
    project(2 * B, R, False)
    near_keys = ((-R, R), (B, R))
    distances(0, B, near_keys, 0)

    @pl.loop(0, pairs)
    def _(hp):
        for b in range(2):
            attend(b * R, near_keys, b * R, hp, False, False)

    n = members * CH
    row_i = lax.broadcasted_iota(jnp.int32, (n, members), 0)
    col_t = lax.broadcasted_iota(jnp.int32, (n, members), 1)
    spread = jnp.where(
        (row_i >= col_t * CH) & (row_i < (col_t + 1) * CH), 1.0, 0.0
    ).astype(BF16)
    half_mix = nn_dot(spread, mix[...]).astype(BF16)
    full_mix = nt_dot(half_mix, spread)
    i2 = lax.broadcasted_iota(jnp.int32, (n, n), 0) & (CH - 1)
    j2 = lax.broadcasted_iota(jnp.int32, (n, n), 1) & (CH - 1)
    KR[...] = jnp.where(i2 == j2, full_mix, 0.0).astype(BF16)

    far_keys = (((-B, R),), ((B + R, R),))
    for b in range(2):
        distances(b * R, R, far_keys[b], b * R)
    for k in range(2):
        for side in range(2):
            halo_arrived(1, side, k)
    project(0, R, False)
    project(2 * B + R, R, False)

    @pl.loop(0, pairs)
    def _(hp):
        for b in range(2):
            attend(b * R, far_keys[b], b * R, hp, False, True)

    loads[1].wait()

    @pl.loop(0, D // tile)
    def _(j):
        cols = pl.ds(pl.multiple_of(j * tile, tile), tile)
        HID[:, cols] = (
            X[B:2 * B, cols].astype(F32) + nn_dot(ATT[...], wo[:, cols])
        ).astype(BF16)

    hid_copy = pltpu.make_async_remote_copy(
        src_ref=HID.at[pl.ds(pl.multiple_of(other * R, R), R)], dst_ref=HS,
        send_sem=hs_sem.at[0], recv_sem=hs_sem.at[1],
        device_id={"tm": sib}, device_id_type=MESH,
    )
    hid_copy.start()
    loads[2].wait()

    @pl.loop(0, C // tile)
    def _(j):
        cols = pl.ds(pl.multiple_of(j * tile, tile), tile)
        BR[:, cols] = nn_dot(HID[...], wd[:, cols]).astype(BF16)

    slot = pl.ds(pl.multiple_of(mine * CH, CH), CH)

    def spread_copy(j):
        p, pg, pc = member(j)
        return pltpu.make_async_remote_copy(
            src_ref=BR.at[pl.ds(pl.multiple_of(pc * R + pg * CH, CH), CH)], dst_ref=RX.at[slot],
            send_sem=a1s.at[j], recv_sem=a1r.at[mine],
            device_id={"tm": chip * 2 + pc, "series": pg}, device_id_type=MESH,
        )

    spreads = [spread_copy(j) for j in range(1, members)]
    for copy in spreads:
        copy.start()
    RX[slot, :] = BR[pl.ds(pl.multiple_of(c * R + g * CH, CH), CH), :]
    for j in range(1, members):
        p, pg, pc = member(j)
        pltpu.make_async_remote_copy(
            src_ref=BR.at[pl.ds(0, CH)], dst_ref=RX.at[pl.ds(pl.multiple_of(p * CH, CH), CH)],
            send_sem=a1s.at[j], recv_sem=a1r.at[p],
            device_id={"tm": chip * 2 + pc, "series": pg}, device_id_type=MESH,
        ).wait_recv()
    mixed = nn_dot(KR[...], RX[...]).astype(BF16)
    CB[...] = mixed.reshape(members, CH, C)

    def back_copy(j):
        pg = lax.rem(g + j, groups)
        return pltpu.make_async_remote_copy(
            src_ref=CB.at[pl.ds(2 * pg, 2)],
            dst_ref=CI.at[:, pl.ds(pl.multiple_of(g * CH, CH), CH), :],
            send_sem=a2s.at[j], recv_sem=a2r.at[g],
            device_id={"series": pg}, device_id_type=MESH,
        )

    backs = [back_copy(j) for j in range(1, groups)]
    for copy in backs:
        copy.start()
    CI[:, pl.ds(pl.multiple_of(g * CH, CH), CH), :] = CB[pl.ds(2 * g, 2)]
    hid_copy.wait_recv()
    loads[3].wait()
    for j in range(1, groups):
        pg = lax.rem(g + j, groups)
        pltpu.make_async_remote_copy(
            src_ref=CB.at[pl.ds(0, 2)],
            dst_ref=CI.at[:, pl.ds(pl.multiple_of(pg * CH, CH), CH), :],
            send_sem=a2s.at[j], recv_sem=a2r.at[pg],
            device_id={"series": pg}, device_id_type=MESH,
        ).wait_recv()

    @pl.loop(0, D // tile)
    def _(j):
        cols = pl.ds(pl.multiple_of(j * tile, tile), tile)
        own_hidden = HID[pl.ds(pl.multiple_of(c * R, R), R), cols]
        out[c, :, cols] = (
            own_hidden.astype(F32) + nn_dot(CI[c], wu[:, cols])
        ).astype(BF16)
        out[other, :, cols] = (
            HS[:, cols].astype(F32) + nn_dot(CI[other], wu[:, cols])
        ).astype(BF16)

    sib_copy.wait_send()
    hid_copy.wait_send()
    for copy in far + spreads + backs:
        copy.wait_send()


def on_device(
    history, lengths, head_window, input_proj, output_proj, mixer_down, mixer_up, series_mix
):
    S, R, D = history.shape
    C = mixer_down.shape[1]
    chips = lax.axis_size("tm") // 2
    groups = lax.axis_size("series")
    members = 2 * groups
    B = 2 * R
    CH = B // members
    smem = pl.BlockSpec(memory_space=pltpu.SMEM)
    vmem = pl.BlockSpec(memory_space=pltpu.VMEM)
    hbm = pl.BlockSpec(memory_space=pl.ANY)
    dma = pltpu.SemaphoreType.DMA
    return pl.pallas_call(
        functools.partial(layer_kernel, (chips, groups)),
        out_shape=jax.ShapeDtypeStruct((S, R, D), BF16),
        in_specs=[smem, smem, vmem, hbm, hbm, hbm, hbm, hbm],
        out_specs=vmem,
        scratch_shapes=[
            pltpu.VMEM((3 * B, D), BF16),
            pltpu.VMEM((B, D), BF16),
            pltpu.VMEM((3 * B, D), BF16),
            pltpu.VMEM((3 * B, 2 * D), BF16),
            pltpu.VMEM((B, D), F32),
            pltpu.VMEM((B, D), F32),
            pltpu.VMEM((B, D), F32),
            pltpu.VMEM((B, B), jnp.int32),
            pltpu.VMEM((B, D), BF16),
            pltpu.VMEM((B, D), BF16),
            pltpu.VMEM((B, C), BF16),
            pltpu.VMEM((members * CH, C), BF16),
            pltpu.VMEM((members * CH, members * CH), BF16),
            pltpu.VMEM((members, CH, C), BF16),
            pltpu.VMEM((2, R, C), BF16),
            pltpu.VMEM((R, D), BF16),
            pltpu.VMEM(input_proj.shape, BF16),
            pltpu.VMEM(output_proj.shape, BF16),
            pltpu.VMEM(mixer_down.shape, BF16),
            pltpu.VMEM(mixer_up.shape, BF16),
            dma((5,)), dma((2,)), dma((2,)), dma((2, 2, 2)), dma((2, 2, 2)),
            dma((members,)), dma((members,)), dma((groups,)), dma((groups,)),
        ],
        compiler_params=pltpu.CompilerParams(
            collective_id=0, has_side_effects=True, vmem_limit_bytes=64 * 1024 * 1024 - 65536
        ),
        name="layer",
    )(lengths, head_window, series_mix, history, input_proj, output_proj, mixer_down, mixer_up)


def solution(mesh):
    in_specs = (P("series", "tm", None), P("series"), P(), P(), P(), P(), P(), P())
    out_specs = P("series", "tm", None)
    return jax.shard_map(
        on_device, mesh=mesh, in_specs=in_specs, out_specs=out_specs, check_vma=False
    )
```

time: 282 us -> 82.9 us (0.29)
  the two profiles are of different devices: /device:TPU:9 before, /device:TPU:1 now
where the time goes in v1:
time: 82.9 us; the launch traced here: 82.8 us
  Pallas kernels  80.5 us (97%)
  local copies, waits for them, and re-layouts  2.26 us (3%)
    pallas_call x1, Pallas kernels, on_device(): pl.pallas_call(functools.partial(layer_kernel, (chips, groups)), out_shap...  80.5 us
    unnamed x1, local copies, waits for them, and re-layouts  2.26 us

profile of v1, /device:TPU:1, one launch (start us, length us, event | category | flops | bytes accessed | tf_op | source)
XLA Modules:
  0.0 82.8 jit_solution(10601012872107121901)
XLA Ops:
  0.0 80.5 %layer.1 = bf16[2,256,1024]{2,1,0:T(8,128)(2,1)} custom-call(s32[2]{0:T(128)} %lengths.1, s32[16]{0:T(128)} %window.1, bf16[16,16]{1,0:T(8,128)(2,1)} %mix.1, bf16[2,256,1024]{2,1,0:T(8,128)(2,1)} %hist.1, bf16[1024,3072]{1,0:T(8,128)(2,1)} %wi_any.1, bf16[1024,1024]{1,0:T(8,128)(2,1)} %wo_any.1, bf16[1024,512]{1,0:T(8,128)(2,1)} %wd_any.1, ...), custom_call_target="tpu_custom_call" | custom-call | tf_op jit(solution)/shard_map/layer/pallas_call | solution.py:376
  80.5 2.3 %copy.10 = bf16[2,256,1024]{2,1,0:T(8,128)(2,1)} copy(bf16[2,256,1024]{2,1,0:T(8,128)(2,1)} %layer.1) | data formatting | bytes 2097152

commit v2 on v1

v2 whole, which is shorter than its diff:
```python
import functools
import math

import jax
import jax.numpy as jnp
from jax import lax
from jax.experimental import pallas as pl
from jax.experimental.pallas import tpu as pltpu
from jax.sharding import PartitionSpec as P

HEAD_SIZE = 64
PAIR = 2 * HEAD_SIZE
NEG = -1e30
FAR = 1 << 20
MESH = pl.DeviceIdType.MESH
BF16 = jnp.bfloat16
F32 = jnp.float32
SCALE = HEAD_SIZE ** -0.5 * math.log2(math.e)


def nt_dot(a, b):
    return lax.dot_general(a, b, (((1,), (1,)), ((), ())), preferred_element_type=F32)


def nn_dot(a, b):
    return jnp.dot(a, b, preferred_element_type=F32)


def layer_kernel(
    dims, lengths, window, mix, hist, wi_any, wo_any, wd_any, wu_any, out,
    X, Q, K, VO, M, L, ACC, DIST, DMID, DOUT, S0, S1, T0, T1, ATT, HID, BR, RX, KR, CB, CI, HS,
    wi, wo, wd, wu,
    loc_sem, sib_sem, hs_sem, rs_sem, rr_sem, a1s, a1r, a2s, a2r,
):
    chips, groups = dims
    members = 2 * groups
    _, R, D = hist.shape
    B = 2 * R
    RC = R // 2
    C = BR.shape[1]
    CH = RC // groups
    pairs = D // PAIR
    me = lax.axis_index("tm")
    g = lax.axis_index("series")
    c = lax.rem(me, 2)
    chip = me // 2
    other = 1 - c
    sib = chip * 2 + other
    mine = g * 2 + c
    rchip = lax.rem(chip + 1, chips)
    lchip = lax.rem(chip + chips - 1, chips)
    total = chips * B
    has_left = chip > 0
    has_right = chip < chips - 1

    def member(j):
        p = lax.rem(mine + j, members)
        return p, p // 2, lax.rem(p, 2)

    barrier = pltpu.get_barrier_semaphore()
    for nchip in (lchip, rchip):
        for core in range(2):
            pl.semaphore_signal(
                barrier, inc=1, device_id={"tm": nchip * 2 + core}, device_id_type=MESH
            )
    for j in range(1, members):
        _, pg, pc = member(j)
        pl.semaphore_signal(
            barrier, inc=1, device_id={"tm": chip * 2 + pc, "series": pg}, device_id_type=MESH
        )
    own_rows = pl.multiple_of(B + c * R, R)
    own_load = pltpu.make_async_copy(hist.at[c], X.at[pl.ds(own_rows, R)], loc_sem.at[0])
    own_load.start()
    loads = [
        pltpu.make_async_copy(src, dst, loc_sem.at[1 + i])
        for i, (src, dst) in enumerate(((wi_any, wi), (wo_any, wo), (wd_any, wd), (wu_any, wu)))
    ]
    loads[0].start()
    pl.semaphore_wait(barrier, 4 + members - 1)

    sib_copy = pltpu.make_async_remote_copy(
        src_ref=hist.at[other], dst_ref=X.at[pl.ds(own_rows, R)],
        send_sem=sib_sem.at[0], recv_sem=sib_sem.at[1],
        device_id={"tm": sib}, device_id_type=MESH,
    )
    sib_copy.start()

    sends = (
        jnp.where(c == 1, has_right, has_left),
        jnp.where(c == 1, has_left, has_right),
    )

    def halo_copy(phase, k, s):
        if phase == 0:
            target = jnp.where(c == 1, rchip, lchip)
            side = 1 - c
            kk = k + c * (1 - 2 * k)
            base = 2 * B + c * (R - 2 * B)
        else:
            target = jnp.where(c == 1, lchip, rchip)
            side = c
            kk = (1 - k) + c * (2 * k - 1)
            base = c * (2 * B + R)
        row = pl.multiple_of(base + kk * RC, RC)
        return pltpu.make_async_remote_copy(
            src_ref=hist.at[s, pl.ds(pl.multiple_of(kk * RC, RC), RC)],
            dst_ref=X.at[pl.ds(row, RC)],
            send_sem=rs_sem.at[phase, k, s], recv_sem=rr_sem.at[phase, side, k],
            device_id={"tm": target * 2 + s}, device_id_type=MESH,
        )

    def halo_row(phase, side, k):
        base = ((R, 2 * B), (0, 2 * B + R))[phase][side]
        return base + ((1 - k) if side == 0 else k) * RC

    def halo_arrived(phase, k):
        for side in range(2):
            @pl.when((has_left, has_right)[side])
            def _():
                pltpu.make_async_remote_copy(
                    src_ref=hist.at[0, pl.ds(0, RC)],
                    dst_ref=X.at[pl.ds(halo_row(phase, side, k), RC)],
                    send_sem=rs_sem.at[phase, k, 0], recv_sem=rr_sem.at[phase, side, k],
                    device_id={"tm": sib}, device_id_type=MESH,
                ).wait_recv()

    def start_halo(phase):
        @pl.when(sends[phase])
        def _():
            for k in range(2):
                for s in range(2):
                    halo_copy(phase, k, s).start()

    def halo_sent(phase, k):
        @pl.when(sends[phase])
        def _():
            for s in range(2):
                halo_copy(phase, k, s).wait_send()

    start_halo(0)
    for load in loads[1:]:
        load.start()

    @pl.when(jnp.logical_not(has_left))
    def _():
        X[0:B, :] = jnp.zeros((B, D), BF16)

    @pl.when(jnp.logical_not(has_right))
    def _():
        X[2 * B:3 * B, :] = jnp.zeros((B, D), BF16)

    for p in range(pairs):
        VO[:, p * 2 * PAIR + PAIR:(p + 1) * 2 * PAIR] = jnp.ones((3 * B, PAIR), BF16)

    tile = 256

    def stacked(ref, rows, cols=slice(None)):
        parts = [ref[first:first + count, cols] for first, count in rows]
        return parts[0] if len(parts) == 1 else jnp.concatenate(parts, axis=0)

    def scatter(ref, rows, cols, value):
        at = 0
        for first, count in rows:
            ref[first:first + count, cols] = value[at:at + count]
            at += count

    def project(rows, with_queries):
        @pl.loop(0, D // tile)
        def _(j):
            cols = pl.ds(pl.multiple_of(j * tile, tile), tile)
            x = stacked(X, rows)
            if with_queries:
                Q[:, cols] = (nn_dot(x, wi[:, cols]) * SCALE).astype(BF16)
            kcols = pl.ds(pl.multiple_of(D + j * tile, tile), tile)
            scatter(K, rows, cols, nn_dot(x, wi[:, kcols]).astype(BF16))
            wcols = pl.ds(pl.multiple_of(2 * D + j * tile, tile), tile)
            values = nn_dot(x, wi[:, wcols]).astype(BF16)
            for i in range(tile // PAIR):
                at = pl.multiple_of((j * (tile // PAIR) + i) * 2 * PAIR, 2 * PAIR)
                scatter(VO, rows, pl.ds(at, PAIR), values[:, i * PAIR:(i + 1) * PAIR])

    length = lengths[c]
    first_valid = total - length

    def distances(ref, at, unit):
        q_first, n, k_ranges = unit[:3]
        column = 0
        for k_first, k_count in k_ranges:
            qi = q_first + lax.broadcasted_iota(jnp.int32, (n, k_count), 0)
            kj = k_first + lax.broadcasted_iota(jnp.int32, (n, k_count), 1)
            kpos = chip * B + kj
            valid = (kpos >= first_valid) & (kpos < total) & (kpos >= 0)
            ref[at:at + n, column:column + k_count] = jnp.where(valid, jnp.abs(qi - kj), FAR)
            column += k_count

    def pair_cols(hp):
        return pl.ds(pl.multiple_of(hp * PAIR, PAIR), PAIR)

    def scores(unit, hp, S, T):
        q_first, n, k_ranges, ref, at = unit
        low = lax.broadcasted_iota(jnp.int32, (n, PAIR), 1) < HEAD_SIZE
        cols = pair_cols(hp)
        q = Q[q_first:q_first + n, cols]
        zero = jnp.zeros_like(q)
        both = jnp.concatenate([jnp.where(low, q, zero), jnp.where(low, zero, q)], axis=0)
        tops = []
        column = 0
        for k_first, k_count in k_ranges:
            s = nt_dot(both, K[B + k_first:B + k_first + k_count, cols])
            dist = ref[at:at + n, column:column + k_count]
            s = jnp.concatenate([
                jnp.where(dist <= window[2 * hp], s[:n], NEG),
                jnp.where(dist <= window[2 * hp + 1], s[n:], NEG),
            ], axis=0)
            S[:2 * n, column:column + k_count] = s
            tops.append(jnp.max(s, axis=1, keepdims=True))
            column += k_count
        top = functools.reduce(jnp.maximum, tops)
        T[:2 * n, :] = jnp.broadcast_to(top, (2 * n, PAIR))

    def values(unit, hp, S, T, first, last):
        q_first, n, k_ranges, _, _ = unit
        low = lax.broadcasted_iota(jnp.int32, (n, PAIR), 1) < HEAD_SIZE
        cols = pair_cols(hp)
        vcols = pl.ds(pl.multiple_of(hp * 2 * PAIR, 2 * PAIR), 2 * PAIR)
        q_rows = slice(q_first, q_first + n)
        top = T[:2 * n, :]
        if not first:
            old = jnp.concatenate([M[hp, 0, q_rows, :], M[hp, 1, q_rows, :]], axis=0)
            top = jnp.maximum(top, old)
        added = None
        column = 0
        for k_first, k_count in k_ranges:
            step = min(PAIR, k_count)
            p = jnp.concatenate([
                jnp.exp2(S[:2 * n, column + i:column + i + step] - top[:, :step]).astype(BF16)
                for i in range(0, k_count, step)
            ], axis=1)
            part = nn_dot(p, VO[B + k_first:B + k_first + k_count, vcols])
            added = part if added is None else added + part
            column += k_count
        acc = jnp.where(low, added[:n, :PAIR], added[n:, :PAIR])
        sums = jnp.where(low, added[:n, PAIR:], added[n:, PAIR:])
        if not first:
            alpha = jnp.exp2(jnp.where(low, old[:n] - top[:n], old[n:] - top[n:]))
            acc = acc + ACC[q_rows, cols] * alpha
            sums = sums + L[q_rows, cols] * alpha
        if last:
            qpos = chip * B + q_first + lax.broadcasted_iota(jnp.int32, (n, PAIR), 0)
            ATT[q_rows, cols] = jnp.where(qpos >= first_valid, acc / sums, 0.0).astype(BF16)
        else:
            M[hp, 0, q_rows, :] = top[:n]
            M[hp, 1, q_rows, :] = top[n:]
            ACC[q_rows, cols] = acc
            L[q_rows, cols] = sums

    def attend(units, first, last):
        scores(units[0], 0, S0, T0)

        @pl.loop(0, pairs)
        def _(hp):
            scores(units[1], hp, S1, T1)
            values(units[0], hp, S0, T0, first, last)
            scores(units[0], jnp.minimum(hp + 1, pairs - 1), S0, T0)
            values(units[1], hp, S1, T1, first, last)

    own_load.wait()
    sib_copy.wait_recv()
    loads[0].wait()
    project([(B, B)], True)
    halo_sent(0, 0)
    start_halo(1)
    own = [(b * R, R, ((0, B),), DIST, b * R) for b in range(2)]
    for unit in own:
        distances(DIST, unit[4], unit)
    attend(own, True, False)

    for k in range(2):
        halo_arrived(0, k)
    project([(R, R), (2 * B, R)], False)
    near = [(b * R, R, ((-R, R), (B, R)), DIST, b * R) for b in range(2)]
    for unit in near:
        distances(DIST, unit[4], unit)
    attend(near, False, False)

    n = members * CH
    row_i = lax.broadcasted_iota(jnp.int32, (n, members), 0)
    col_t = lax.broadcasted_iota(jnp.int32, (n, members), 1)
    spread = jnp.where(
        (row_i >= col_t * CH) & (row_i < (col_t + 1) * CH), 1.0, 0.0
    ).astype(BF16)
    half_mix = nn_dot(spread, mix[...]).astype(BF16)
    full_mix = nt_dot(half_mix, spread)
    i2 = lax.broadcasted_iota(jnp.int32, (n, n), 0) & (CH - 1)
    j2 = lax.broadcasted_iota(jnp.int32, (n, n), 1) & (CH - 1)
    KR[...] = jnp.where(i2 == j2, full_mix, 0.0).astype(BF16)

    far_mid = [
        (RC, RC, ((-B + RC, RC),), DMID, 0),
        (R, RC, ((B + R, RC),), DMID, RC),
    ]
    far_out = [
        (0, RC, ((-B, R),), DOUT, 0),
        (R + RC, RC, ((B + R, R),), DOUT, RC),
    ]
    for unit in far_mid + far_out:
        distances(unit[3], unit[4], unit)

    def rows_of(group, core):
        return (RC + core * RC) if group == 0 else core * (R + RC)

    def spread_copy(group, j):
        p, pg, pc = member(j)
        row = pl.multiple_of(rows_of(group, pc) + pg * CH, CH)
        return pltpu.make_async_remote_copy(
            src_ref=BR.at[pl.ds(row, CH)],
            dst_ref=RX.at[group, pl.ds(pl.multiple_of(mine * CH, CH), CH)],
            send_sem=a1s.at[group, j], recv_sem=a1r.at[group, mine],
            device_id={"tm": chip * 2 + pc, "series": pg}, device_id_type=MESH,
        )

    def spread_arrived(group, j):
        p, pg, pc = member(j)
        pltpu.make_async_remote_copy(
            src_ref=BR.at[pl.ds(0, CH)],
            dst_ref=RX.at[group, pl.ds(pl.multiple_of(p * CH, CH), CH)],
            send_sem=a1s.at[group, j], recv_sem=a1r.at[group, p],
            device_id={"tm": chip * 2 + pc, "series": pg}, device_id_type=MESH,
        ).wait_recv()

    def local_rows(group, core):
        return rows_of(group, core) - core * R

    def back_copy(group, j):
        pg = lax.rem(g + j, groups)
        row = pl.multiple_of(local_rows(group, c) + g * CH, CH)
        return pltpu.make_async_remote_copy(
            src_ref=CB.at[group, pl.ds(2 * pg, 2)],
            dst_ref=CI.at[:, pl.ds(row, CH), :],
            send_sem=a2s.at[group, j], recv_sem=a2r.at[group, g],
            device_id={"series": pg}, device_id_type=MESH,
        )

    def back_arrived(group, j):
        pg = lax.rem(g + j, groups)
        row = pl.multiple_of(local_rows(group, c) + pg * CH, CH)
        pltpu.make_async_remote_copy(
            src_ref=CB.at[group, pl.ds(0, 2)],
            dst_ref=CI.at[:, pl.ds(row, CH), :],
            send_sem=a2s.at[group, j], recv_sem=a2r.at[group, pg],
            device_id={"series": pg}, device_id_type=MESH,
        ).wait_recv()

    def hidden_copy(group):
        src = pl.multiple_of(rows_of(group, other), RC)
        dst = pl.multiple_of(local_rows(group, other), RC)
        return pltpu.make_async_remote_copy(
            src_ref=HID.at[pl.ds(src, RC)], dst_ref=HS.at[pl.ds(dst, RC)],
            send_sem=hs_sem.at[group, 0], recv_sem=hs_sem.at[group, 1],
            device_id={"tm": sib}, device_id_type=MESH,
        )

    def finish_rows(group, rows):
        @pl.loop(0, D // tile)
        def _(j):
            cols = pl.ds(pl.multiple_of(j * tile, tile), tile)
            own_x = stacked(X, [(B + first, count) for first, count in rows], cols)
            update = nn_dot(stacked(ATT, rows), wo[:, cols])
            scatter(HID, rows, cols, (own_x.astype(F32) + update).astype(BF16))

        hidden_copy(group).start()

        @pl.loop(0, C // tile)
        def _(j):
            cols = pl.ds(pl.multiple_of(j * tile, tile), tile)
            scatter(BR, rows, cols, nn_dot(stacked(HID, rows), wd[:, cols]).astype(BF16))

        for j in range(1, members):
            spread_copy(group, j).start()
        row = pl.multiple_of(rows_of(group, c) + g * CH, CH)
        RX[group, pl.ds(pl.multiple_of(mine * CH, CH), CH), :] = BR[pl.ds(row, CH), :]

    def mix_rows(group):
        for j in range(1, members):
            spread_arrived(group, j)
        CB[group] = nn_dot(KR[...], RX[group]).astype(BF16).reshape(members, CH, C)
        for j in range(1, groups):
            back_copy(group, j).start()
        row = pl.multiple_of(local_rows(group, c) + g * CH, CH)
        CI[:, pl.ds(row, CH), :] = CB[group, pl.ds(2 * g, 2)]

    def put_rows(group):
        hidden_copy(group).wait_recv()
        for j in range(1, groups):
            back_arrived(group, j)
        from_row = pl.multiple_of(rows_of(group, c), RC)
        at_row = pl.multiple_of(local_rows(group, c), RC)
        rows = pl.ds(at_row, RC)

        @pl.loop(0, D // tile)
        def _(j):
            cols = pl.ds(pl.multiple_of(j * tile, tile), tile)
            sums = jnp.concatenate([CI[c, rows, :], CI[other, rows, :]], axis=0)
            update = nn_dot(sums, wu[:, cols])
            out[c, rows, cols] = (
                HID[pl.ds(from_row, RC), cols].astype(F32) + update[:RC]
            ).astype(BF16)
            out[other, rows, cols] = (HS[rows, cols].astype(F32) + update[RC:]).astype(BF16)

    mid_rows = [(RC, R)]
    out_rows = [(0, RC), (R + RC, RC)]
    halo_arrived(1, 0)
    project([(halo_row(1, 0, 0), RC), (halo_row(1, 1, 0), RC)], False)
    attend(far_mid, False, True)
    loads[1].wait()
    loads[2].wait()
    finish_rows(0, mid_rows)
    halo_arrived(1, 1)
    project([(halo_row(1, 0, 1), RC), (halo_row(1, 1, 1), RC)], False)
    attend(far_out, False, True)
    finish_rows(1, out_rows)
    mix_rows(0)
    mix_rows(1)
    loads[3].wait()
    put_rows(0)
    put_rows(1)

    sib_copy.wait_send()
    halo_sent(0, 1)
    for k in range(2):
        halo_sent(1, k)
    for group in range(2):
        hidden_copy(group).wait_send()
        for j in range(1, members):
            spread_copy(group, j).wait_send()
        for j in range(1, groups):
            back_copy(group, j).wait_send()


def on_device(
    history, lengths, head_window, input_proj, output_proj, mixer_down, mixer_up, series_mix
):
    S, R, D = history.shape
    C = mixer_down.shape[1]
    chips = lax.axis_size("tm") // 2
    groups = lax.axis_size("series")
    members = 2 * groups
    B = 2 * R
    RC = R // 2
    CH = RC // groups
    pairs = D // PAIR
    smem = pl.BlockSpec(memory_space=pltpu.SMEM)
    vmem = pl.BlockSpec(memory_space=pltpu.VMEM)
    hbm = pl.BlockSpec(memory_space=pl.ANY)
    dma = pltpu.SemaphoreType.DMA
    return pl.pallas_call(
        functools.partial(layer_kernel, (chips, groups)),
        out_shape=jax.ShapeDtypeStruct((S, R, D), BF16),
        in_specs=[smem, smem, vmem, hbm, hbm, hbm, hbm, hbm],
        out_specs=vmem,
        scratch_shapes=[
            pltpu.VMEM((3 * B, D), BF16),
            pltpu.VMEM((B, D), BF16),
            pltpu.VMEM((3 * B, D), BF16),
            pltpu.VMEM((3 * B, 2 * D), BF16),
            pltpu.VMEM((pairs, 2, B, PAIR), F32),
            pltpu.VMEM((B, D), F32),
            pltpu.VMEM((B, D), F32),
            pltpu.VMEM((B, B), jnp.int32),
            pltpu.VMEM((R, RC), jnp.int32),
            pltpu.VMEM((R, R), jnp.int32),
            pltpu.VMEM((B, B), F32),
            pltpu.VMEM((B, B), F32),
            pltpu.VMEM((B, PAIR), F32),
            pltpu.VMEM((B, PAIR), F32),
            pltpu.VMEM((B, D), BF16),
            pltpu.VMEM((B, D), BF16),
            pltpu.VMEM((B, C), BF16),
            pltpu.VMEM((2, members * CH, C), BF16),
            pltpu.VMEM((members * CH, members * CH), BF16),
            pltpu.VMEM((2, members, CH, C), BF16),
            pltpu.VMEM((2, R, C), BF16),
            pltpu.VMEM((R, D), BF16),
            pltpu.VMEM(input_proj.shape, BF16),
            pltpu.VMEM(output_proj.shape, BF16),
            pltpu.VMEM(mixer_down.shape, BF16),
            pltpu.VMEM(mixer_up.shape, BF16),
            dma((5,)), dma((2,)), dma((2, 2)), dma((2, 2, 2)), dma((2, 2, 2)),
            dma((2, members)), dma((2, members)), dma((2, groups)), dma((2, groups)),
        ],
        compiler_params=pltpu.CompilerParams(
            collective_id=0, has_side_effects=True, vmem_limit_bytes=64 * 1024 * 1024 - 65536
        ),
        name="layer",
    )(lengths, head_window, series_mix, history, input_proj, output_proj, mixer_down, mixer_up)


def solution(mesh):
    in_specs = (P("series", "tm", None), P("series"), P(), P(), P(), P(), P(), P())
    out_specs = P("series", "tm", None)
    return jax.shard_map(
        on_device, mesh=mesh, in_specs=in_specs, out_specs=out_specs, check_vma=False
    )
```

time: 82.9 us -> 72 us (0.87)
  the two profiles are of different devices: /device:TPU:1 before, /device:TPU:9 now
where the time goes in v2:
time: 72 us; the launch traced here: 70.9 us
  Pallas kernels  68.6 us (95%)
  local copies, waits for them, and re-layouts  2.26 us (3%)
    pallas_call x1, Pallas kernels, on_device(): pl.pallas_call(functools.partial(layer_kernel, (chips, groups)), out_shap...  68.6 us
    unnamed x1, local copies, waits for them, and re-layouts  2.26 us

profile of v2, /device:TPU:9, one launch (start us, length us, event | category | flops | bytes accessed | tf_op | source)
XLA Modules:
  0.0 70.9 jit_solution(10113445744684801775)
XLA Ops:
  0.0 68.6 %layer.1 = bf16[2,256,1024]{2,1,0:T(8,128)(2,1)} custom-call(s32[2]{0:T(128)} %lengths.1, s32[16]{0:T(128)} %window.1, bf16[16,16]{1,0:T(8,128)(2,1)} %mix.1, bf16[2,256,1024]{2,1,0:T(8,128)(2,1)} %hist.1, bf16[1024,3072]{1,0:T(8,128)(2,1)} %wi_any.1, bf16[1024,1024]{1,0:T(8,128)(2,1)} %wo_any.1, bf16[1024,512]{1,0:T(8,128)(2,1)} %wd_any.1, ...), custom_call_target="tpu_custom_call" | custom-call | tf_op jit(solution)/shard_map/layer/pallas_call | solution.py:456
  68.6 2.3 %copy.10 = bf16[2,256,1024]{2,1,0:T(8,128)(2,1)} copy(bf16[2,256,1024]{2,1,0:T(8,128)(2,1)} %layer.1) | data formatting | bytes 2097152

commit v3 on v2

--- a/solution.py
+++ b/solution.py
@@ -27,9 +27,9 @@
 
 
 def layer_kernel(
-    dims, lengths, window, mix, hist, wi_any, wo_any, wd_any, wu_any, out,
-    X, Q, K, VO, M, L, ACC, DIST, DMID, DOUT, S0, S1, T0, T1, ATT, HID, BR, RX, KR, CB, CI, HS,
-    wi, wo, wd, wu,
+    dims, lengths, window, mix, hist, wi_any, wo_any, wd_any, hid_out, mix_out,
+    X, Q, K, VO, M, L, ACC, DIST, DMID, DOUT, S0, S1, T0, T1, ATT, HID, BR, RX, KR, CB,
+    wi, wo, wd,
     loc_sem, sib_sem, hs_sem, rs_sem, rr_sem, a1s, a1r, a2s, a2r,
 ):
     chips, groups = dims
@@ -68,12 +68,12 @@
         pl.semaphore_signal(
             barrier, inc=1, device_id={"tm": chip * 2 + pc, "series": pg}, device_id_type=MESH
         )
-    own_rows = pl.multiple_of(B + c * R, R)
+    own_rows = pl.multiple_of(c * R, R)
     own_load = pltpu.make_async_copy(hist.at[c], X.at[pl.ds(own_rows, R)], loc_sem.at[0])
     own_load.start()
     loads = [
         pltpu.make_async_copy(src, dst, loc_sem.at[1 + i])
-        for i, (src, dst) in enumerate(((wi_any, wi), (wo_any, wo), (wd_any, wd), (wu_any, wu)))
+        for i, (src, dst) in enumerate(((wi_any, wi), (wo_any, wo), (wd_any, wd)))
     ]
     loads[0].start()
     pl.semaphore_wait(barrier, 4 + members - 1)
@@ -95,12 +95,12 @@
             target = jnp.where(c == 1, rchip, lchip)
             side = 1 - c
             kk = k + c * (1 - 2 * k)
-            base = 2 * B + c * (R - 2 * B)
+            base = B + side * R
         else:
             target = jnp.where(c == 1, lchip, rchip)
             side = c
             kk = (1 - k) + c * (2 * k - 1)
-            base = c * (2 * B + R)
+            base = 2 * B + side * R
         row = pl.multiple_of(base + kk * RC, RC)
         return pltpu.make_async_remote_copy(
             src_ref=hist.at[s, pl.ds(pl.multiple_of(kk * RC, RC), RC)],
@@ -110,8 +110,7 @@
         )
 
     def halo_row(phase, side, k):
-        base = ((R, 2 * B), (0, 2 * B + R))[phase][side]
-        return base + ((1 - k) if side == 0 else k) * RC
+        return (phase + 1) * B + side * R + ((1 - k) if side == 0 else k) * RC
 
     def halo_arrived(phase, k):
         for side in range(2):
@@ -143,11 +142,13 @@
 
     @pl.when(jnp.logical_not(has_left))
     def _():
-        X[0:B, :] = jnp.zeros((B, D), BF16)
+        for phase in range(1, 3):
+            X[phase * B:phase * B + R, :] = jnp.zeros((R, D), BF16)
 
     @pl.when(jnp.logical_not(has_right))
     def _():
-        X[2 * B:3 * B, :] = jnp.zeros((B, D), BF16)
+        for phase in range(1, 3):
+            X[phase * B + R:(phase + 1) * B, :] = jnp.zeros((R, D), BF16)
 
     for p in range(pairs):
         VO[:, p * 2 * PAIR + PAIR:(p + 1) * 2 * PAIR] = jnp.ones((3 * B, PAIR), BF16)
@@ -182,10 +183,10 @@
     length = lengths[c]
     first_valid = total - length
 
-    def distances(ref, at, unit):
-        q_first, n, k_ranges = unit[:3]
+    def distances(unit):
+        q_first, n, _, segments, ref, at = unit
         column = 0
-        for k_first, k_count in k_ranges:
+        for k_first, k_count in segments:
             qi = q_first + lax.broadcasted_iota(jnp.int32, (n, k_count), 0)
             kj = k_first + lax.broadcasted_iota(jnp.int32, (n, k_count), 1)
             kpos = chip * B + kj
@@ -196,49 +197,41 @@
     def pair_cols(hp):
         return pl.ds(pl.multiple_of(hp * PAIR, PAIR), PAIR)
 
-    def scores(unit, hp, S, T):
-        q_first, n, k_ranges, ref, at = unit
+    def scores(unit, hp, S, T, r0=0):
+        q_first, n, k_row, segments, ref, at = unit
+        count = sum(k_count for _, k_count in segments)
         low = lax.broadcasted_iota(jnp.int32, (n, PAIR), 1) < HEAD_SIZE
         cols = pair_cols(hp)
         q = Q[q_first:q_first + n, cols]
         zero = jnp.zeros_like(q)
         both = jnp.concatenate([jnp.where(low, q, zero), jnp.where(low, zero, q)], axis=0)
-        tops = []
-        column = 0
-        for k_first, k_count in k_ranges:
-            s = nt_dot(both, K[B + k_first:B + k_first + k_count, cols])
-            dist = ref[at:at + n, column:column + k_count]
-            s = jnp.concatenate([
-                jnp.where(dist <= window[2 * hp], s[:n], NEG),
-                jnp.where(dist <= window[2 * hp + 1], s[n:], NEG),
-            ], axis=0)
-            S[:2 * n, column:column + k_count] = s
-            tops.append(jnp.max(s, axis=1, keepdims=True))
-            column += k_count
-        top = functools.reduce(jnp.maximum, tops)
-        T[:2 * n, :] = jnp.broadcast_to(top, (2 * n, PAIR))
-
-    def values(unit, hp, S, T, first, last):
-        q_first, n, k_ranges, _, _ = unit
+        s = nt_dot(both, K[k_row:k_row + count, cols])
+        dist = ref[at:at + n, :count]
+        s = jnp.concatenate([
+            jnp.where(dist <= window[2 * hp], s[:n], NEG),
+            jnp.where(dist <= window[2 * hp + 1], s[n:], NEG),
+        ], axis=0)
+        S[r0:r0 + 2 * n, :count] = s
+        top = jnp.max(s, axis=1, keepdims=True)
+        T[r0:r0 + 2 * n, :] = jnp.broadcast_to(top, (2 * n, PAIR))
+
+    def values(unit, hp, S, T, first, last, r0=0):
+        q_first, n, k_row, segments, _, _ = unit
+        count = sum(k_count for _, k_count in segments)
         low = lax.broadcasted_iota(jnp.int32, (n, PAIR), 1) < HEAD_SIZE
         cols = pair_cols(hp)
         vcols = pl.ds(pl.multiple_of(hp * 2 * PAIR, 2 * PAIR), 2 * PAIR)
         q_rows = slice(q_first, q_first + n)
-        top = T[:2 * n, :]
+        top = T[r0:r0 + 2 * n, :]
         if not first:
             old = jnp.concatenate([M[hp, 0, q_rows, :], M[hp, 1, q_rows, :]], axis=0)
             top = jnp.maximum(top, old)
-        added = None
-        column = 0
-        for k_first, k_count in k_ranges:
-            step = min(PAIR, k_count)
-            p = jnp.concatenate([
-                jnp.exp2(S[:2 * n, column + i:column + i + step] - top[:, :step]).astype(BF16)
-                for i in range(0, k_count, step)
-            ], axis=1)
-            part = nn_dot(p, VO[B + k_first:B + k_first + k_count, vcols])
-            added = part if added is None else added + part
-            column += k_count
+        step = min(PAIR, count)
+        p = jnp.concatenate([
+            jnp.exp2(S[r0:r0 + 2 * n, i:i + step] - top[:, :step]).astype(BF16)
+            for i in range(0, count, step)
+        ], axis=1)
+        added = nn_dot(p, VO[k_row:k_row + count, vcols])
         acc = jnp.where(low, added[:n, :PAIR], added[n:, :PAIR])
         sums = jnp.where(low, added[:n, PAIR:], added[n:, PAIR:])
         if not first:
@@ -255,32 +248,59 @@
             L[q_rows, cols] = sums
 
     def attend(units, first, last):
-        scores(units[0], 0, S0, T0)
-
-        @pl.loop(0, pairs)
-        def _(hp):
-            scores(units[1], hp, S1, T1)
-            values(units[0], hp, S0, T0, first, last)
-            scores(units[0], jnp.minimum(hp + 1, pairs - 1), S0, T0)
-            values(units[1], hp, S1, T1, first, last)
+        if len(units) == 4:
+            batches = [
+                [(unit, 0, 2 * RC * b) for b, unit in enumerate(units[2 * i:2 * i + 2])]
+                for i in range(2)
+            ]
+            step = 1
+        elif units[0][1] == R:
+            batches = [[(units[0], 0, 0)], [(units[1], 0, 0)]]
+            step = 1
+        else:
+            batches = [[(unit, i, 2 * RC * b) for b, unit in enumerate(units)] for i in range(2)]
+            step = 2
+
+        def all_scores(batch, hp, S, T):
+            for unit, plus, r0 in batch:
+                scores(unit, hp + plus, S, T, r0)
+
+        def all_values(batch, hp, S, T):
+            for unit, plus, r0 in batch:
+                values(unit, hp + plus, S, T, first, last, r0)
+
+        all_scores(batches[0], 0, S0, T0)
+
+        @pl.loop(0, pairs // step)
+        def _(i):
+            hp = i * step
+            all_scores(batches[1], hp, S1, T1)
+            all_values(batches[0], hp, S0, T0)
+            all_scores(batches[0], jnp.minimum(hp + step, pairs - step), S0, T0)
+            all_values(batches[1], hp, S1, T1)
 
     own_load.wait()
     sib_copy.wait_recv()
     loads[0].wait()
-    project([(B, B)], True)
+    project([(0, B)], True)
     halo_sent(0, 0)
     start_halo(1)
-    own = [(b * R, R, ((0, B),), DIST, b * R) for b in range(2)]
+    own = [(b * R, R, 0, ((0, B),), DIST, b * R) for b in range(2)]
     for unit in own:
-        distances(DIST, unit[4], unit)
+        distances(unit)
     attend(own, True, False)
 
     for k in range(2):
         halo_arrived(0, k)
-    project([(R, R), (2 * B, R)], False)
-    near = [(b * R, R, ((-R, R), (B, R)), DIST, b * R) for b in range(2)]
+    project([(B, B)], False)
+    near = [
+        (0, RC, B, ((-R, R), (B, RC)), DIST, 0),
+        (RC, RC, B, ((-R, R), (B, R)), DIST, RC),
+        (R, RC, B, ((-R, R), (B, R)), DIST, R),
+        (R + RC, RC, B + RC, ((-RC, RC), (B, R)), DIST, R + RC),
+    ]
     for unit in near:
-        distances(DIST, unit[4], unit)
+        distances(unit)
     attend(near, False, False)
 
     n = members * CH
@@ -296,15 +316,15 @@
     KR[...] = jnp.where(i2 == j2, full_mix, 0.0).astype(BF16)
 
     far_mid = [
-        (RC, RC, ((-B + RC, RC),), DMID, 0),
-        (R, RC, ((B + R, RC),), DMID, RC),
+        (RC, RC, 2 * B + RC, ((-B + RC, RC),), DMID, 0),
+        (R, RC, 2 * B + R, ((B + R, RC),), DMID, RC),
     ]
     far_out = [
-        (0, RC, ((-B, R),), DOUT, 0),
-        (R + RC, RC, ((B + R, R),), DOUT, RC),
+        (0, RC, 2 * B, ((-B, R),), DOUT, 0),
+        (R + RC, RC, 2 * B + R, ((B + R, R),), DOUT, RC),
     ]
     for unit in far_mid + far_out:
-        distances(unit[3], unit[4], unit)
+        distances(unit)
 
     def rows_of(group, core):
         return (RC + core * RC) if group == 0 else core * (R + RC)
@@ -336,7 +356,7 @@
         row = pl.multiple_of(local_rows(group, c) + g * CH, CH)
         return pltpu.make_async_remote_copy(
             src_ref=CB.at[group, pl.ds(2 * pg, 2)],
-            dst_ref=CI.at[:, pl.ds(row, CH), :],
+            dst_ref=mix_out.at[:, pl.ds(row, CH), :],
             send_sem=a2s.at[group, j], recv_sem=a2r.at[group, g],
             device_id={"series": pg}, device_id_type=MESH,
         )
@@ -346,7 +366,7 @@
         row = pl.multiple_of(local_rows(group, c) + pg * CH, CH)
         pltpu.make_async_remote_copy(
             src_ref=CB.at[group, pl.ds(0, 2)],
-            dst_ref=CI.at[:, pl.ds(row, CH), :],
+            dst_ref=mix_out.at[:, pl.ds(row, CH), :],
             send_sem=a2s.at[group, j], recv_sem=a2r.at[group, pg],
             device_id={"series": pg}, device_id_type=MESH,
         ).wait_recv()
@@ -355,20 +375,34 @@
         src = pl.multiple_of(rows_of(group, other), RC)
         dst = pl.multiple_of(local_rows(group, other), RC)
         return pltpu.make_async_remote_copy(
-            src_ref=HID.at[pl.ds(src, RC)], dst_ref=HS.at[pl.ds(dst, RC)],
+            src_ref=HID.at[pl.ds(src, RC)], dst_ref=hid_out.at[c, pl.ds(dst, RC)],
             send_sem=hs_sem.at[group, 0], recv_sem=hs_sem.at[group, 1],
             device_id={"tm": sib}, device_id_type=MESH,
+        )
+
+    def hidden_keep(group):
+        src = pl.multiple_of(rows_of(group, c), RC)
+        dst = pl.multiple_of(local_rows(group, c), RC)
+        return pltpu.make_async_copy(
+            HID.at[pl.ds(src, RC)], hid_out.at[c, pl.ds(dst, RC)], loc_sem.at[4 + group]
+        )
+
+    def mixed_keep(group):
+        row = pl.multiple_of(local_rows(group, c) + g * CH, CH)
+        return pltpu.make_async_copy(
+            CB.at[group, pl.ds(2 * g, 2)], mix_out.at[:, pl.ds(row, CH), :], loc_sem.at[6 + group]
         )
 
     def finish_rows(group, rows):
         @pl.loop(0, D // tile)
         def _(j):
             cols = pl.ds(pl.multiple_of(j * tile, tile), tile)
-            own_x = stacked(X, [(B + first, count) for first, count in rows], cols)
+            own_x = stacked(X, rows, cols)
             update = nn_dot(stacked(ATT, rows), wo[:, cols])
             scatter(HID, rows, cols, (own_x.astype(F32) + update).astype(BF16))
 
         hidden_copy(group).start()
+        hidden_keep(group).start()
 
         @pl.loop(0, C // tile)
         def _(j):
@@ -386,31 +420,12 @@
         CB[group] = nn_dot(KR[...], RX[group]).astype(BF16).reshape(members, CH, C)
         for j in range(1, groups):
             back_copy(group, j).start()
-        row = pl.multiple_of(local_rows(group, c) + g * CH, CH)
-        CI[:, pl.ds(row, CH), :] = CB[group, pl.ds(2 * g, 2)]
-
-    def put_rows(group):
-        hidden_copy(group).wait_recv()
-        for j in range(1, groups):
-            back_arrived(group, j)
-        from_row = pl.multiple_of(rows_of(group, c), RC)
-        at_row = pl.multiple_of(local_rows(group, c), RC)
-        rows = pl.ds(at_row, RC)
-
-        @pl.loop(0, D // tile)
-        def _(j):
-            cols = pl.ds(pl.multiple_of(j * tile, tile), tile)
-            sums = jnp.concatenate([CI[c, rows, :], CI[other, rows, :]], axis=0)
-            update = nn_dot(sums, wu[:, cols])
-            out[c, rows, cols] = (
-                HID[pl.ds(from_row, RC), cols].astype(F32) + update[:RC]
-            ).astype(BF16)
-            out[other, rows, cols] = (HS[rows, cols].astype(F32) + update[RC:]).astype(BF16)
+        mixed_keep(group).start()
 
     mid_rows = [(RC, R)]
     out_rows = [(0, RC), (R + RC, RC)]
     halo_arrived(1, 0)
-    project([(halo_row(1, 0, 0), RC), (halo_row(1, 1, 0), RC)], False)
+    project([(2 * B + RC, R)], False)
     attend(far_mid, False, True)
     loads[1].wait()
     loads[2].wait()
@@ -421,9 +436,12 @@
     finish_rows(1, out_rows)
     mix_rows(0)
     mix_rows(1)
-    loads[3].wait()
-    put_rows(0)
-    put_rows(1)
+    for group in range(2):
+        hidden_copy(group).wait_recv()
+        hidden_keep(group).wait()
+        mixed_keep(group).wait()
+        for j in range(1, groups):
+            back_arrived(group, j)
 
     sib_copy.wait_send()
     halo_sent(0, 1)
@@ -453,11 +471,13 @@
     vmem = pl.BlockSpec(memory_space=pltpu.VMEM)
     hbm = pl.BlockSpec(memory_space=pl.ANY)
     dma = pltpu.SemaphoreType.DMA
-    return pl.pallas_call(
+    hidden, mixed = pl.pallas_call(
         functools.partial(layer_kernel, (chips, groups)),
-        out_shape=jax.ShapeDtypeStruct((S, R, D), BF16),
-        in_specs=[smem, smem, vmem, hbm, hbm, hbm, hbm, hbm],
-        out_specs=vmem,
+        out_shape=(
+            jax.ShapeDtypeStruct((S, R, D), BF16), jax.ShapeDtypeStruct((S, R, C), BF16)
+        ),
+        in_specs=[smem, smem, vmem, hbm, hbm, hbm, hbm],
+        out_specs=(hbm, hbm),
         scratch_shapes=[
             pltpu.VMEM((3 * B, D), BF16),
             pltpu.VMEM((B, D), BF16),
@@ -479,20 +499,19 @@
             pltpu.VMEM((2, members * CH, C), BF16),
             pltpu.VMEM((members * CH, members * CH), BF16),
             pltpu.VMEM((2, members, CH, C), BF16),
-            pltpu.VMEM((2, R, C), BF16),
-            pltpu.VMEM((R, D), BF16),
             pltpu.VMEM(input_proj.shape, BF16),
             pltpu.VMEM(output_proj.shape, BF16),
             pltpu.VMEM(mixer_down.shape, BF16),
-            pltpu.VMEM(mixer_up.shape, BF16),
-            dma((5,)), dma((2,)), dma((2, 2)), dma((2, 2, 2)), dma((2, 2, 2)),
+            dma((8,)), dma((2,)), dma((2, 2)), dma((2, 2, 2)), dma((2, 2, 2)),
             dma((2, members)), dma((2, members)), dma((2, groups)), dma((2, groups)),
         ],
         compiler_params=pltpu.CompilerParams(
             collective_id=0, has_side_effects=True, vmem_limit_bytes=64 * 1024 * 1024 - 65536
         ),
         name="layer",
-    )(lengths, head_window, series_mix, history, input_proj, output_proj, mixer_down, mixer_up)
+    )(lengths, head_window, series_mix, history, input_proj, output_proj, mixer_down)
+    update = jnp.einsum("spc,cd->spd", mixed, mixer_up, preferred_element_type=F32)
+    return (hidden.astype(F32) + update).astype(BF16)
 
 
 def solution(mesh):

time: 72 us -> 69.6 us (0.967)
  Pallas kernels: 68.6 us -> 65.1 us
  matrix products: 0 us -> 3.39 us
  local copies, waits for them, and re-layouts: 2.26 us -> 0 us
    pallas_call x1, Pallas kernels: 68.6 us -> 65.1 us  [on_device(): pl.pallas_call(functools.partial(layer_kernel, (chips, groups)), out_shap...]
    dot_general x0 -> x1, matrix products: none -> 3.39 us  [on_device(): jnp.einsum('spc,cd->spd', mixed, mixer_up, preferred_element_type=F32)]
    unnamed x1 -> x0, local copies, waits for them, and re-layouts: 2.26 us -> none
where the time goes in v3:
time: 69.6 us; the launch traced here: 68.5 us
  Pallas kernels  65.1 us (94%)
  matrix products  3.39 us (5%)
    pallas_call x1, Pallas kernels, on_device(): pl.pallas_call(functools.partial(layer_kernel, (chips, groups)), out_shap...  65.1 us
    dot_general x1, matrix products, on_device(): jnp.einsum('spc,cd->spd', mixed, mixer_up, preferred_element_type=F32)  3.39 us

profile of v3, /device:TPU:9, one launch (start us, length us, event | category | flops | bytes accessed | tf_op | source)
XLA Modules:
  0.0 68.5 jit_solution(10931072392030623102)
XLA Ops:
  0.0 65.1 %layer.1 = (bf16[2,256,1024]{2,1,0:T(8,128)(2,1)}, bf16[2,256,512]{2,1,0:T(8,128)(2,1)}) custom-call(s32[2]{0:T(128)} %lengths.1, s32[16]{0:T(128)} %window.1, bf16[16,16]{1,0:T(8,128)(2,1)} %mix.1, bf16[2,256,1024]{2,1,0:T(8,128)(2,1)} %hist.1, bf16[1024,3072]{1,0:T(8,128)(2,1)} %wi_any.1, bf16[1024,1024]{1,0:T(8,128)(2,1)} %wo_any.1, bf16[1024,512]{1,0:T(8,128)(2,1)} %wd_any.1), custom_call_target="tpu_custom_call" | custom-call | tf_op jit(solution)/shard_map/layer/pallas_call | solution.py:474
  65.2 3.4 %add_convert_fusion = bf16[2,256,1024]{2,1,0:T(8,128)(2,1)} fusion(bf16[2,256,1024]{2,1,0:T(8,128)(2,1)} %get-tuple-element.7, bf16[2,256,512]{2,1,0:T(8,128)(2,1)} %get-tuple-element.8, bf16[512,1024]{1,0:T(8,128)(2,1)} %param.14), kind=kOutput, calls=%fused_computation | convolution fusion | flops 538443776 | bytes 3670016 | tf_op jit(solution)/shard_map/spc,cd->spd/dot_general | solution.py:513

commit v4 on v3

--- a/solution.py
+++ b/solution.py
@@ -28,7 +28,7 @@
 
 def layer_kernel(
     dims, lengths, window, mix, hist, wi_any, wo_any, wd_any, hid_out, mix_out,
-    X, Q, K, VO, M, L, ACC, DIST, DMID, DOUT, S0, S1, T0, T1, ATT, HID, BR, RX, KR, CB,
+    X, Q, K, VO, M, L, ACC, DIST, DNO, DMID, DOUT, S0, S1, T0, T1, ATT, HID, BR, RX, KR, CB,
     wi, wo, wd,
     loc_sem, sib_sem, hs_sem, rs_sem, rr_sem, a1s, a1r, a2s, a2r,
 ):
@@ -156,13 +156,13 @@
     tile = 256
 
     def stacked(ref, rows, cols=slice(None)):
-        parts = [ref[first:first + count, cols] for first, count in rows]
+        parts = [ref[pl.ds(first, count), cols] for first, count in rows]
         return parts[0] if len(parts) == 1 else jnp.concatenate(parts, axis=0)
 
     def scatter(ref, rows, cols, value):
         at = 0
         for first, count in rows:
-            ref[first:first + count, cols] = value[at:at + count]
+            ref[pl.ds(first, count), cols] = value[at:at + count]
             at += count
 
     def project(rows, with_queries):
@@ -171,7 +171,7 @@
             cols = pl.ds(pl.multiple_of(j * tile, tile), tile)
             x = stacked(X, rows)
             if with_queries:
-                Q[:, cols] = (nn_dot(x, wi[:, cols]) * SCALE).astype(BF16)
+                scatter(Q, rows, cols, (nn_dot(x, wi[:, cols]) * SCALE).astype(BF16))
             kcols = pl.ds(pl.multiple_of(D + j * tile, tile), tile)
             scatter(K, rows, cols, nn_dot(x, wi[:, kcols]).astype(BF16))
             wcols = pl.ds(pl.multiple_of(2 * D + j * tile, tile), tile)
@@ -198,14 +198,15 @@
         return pl.ds(pl.multiple_of(hp * PAIR, PAIR), PAIR)
 
     def scores(unit, hp, S, T, r0=0):
-        q_first, n, k_row, segments, ref, at = unit
-        count = sum(k_count for _, k_count in segments)
+        q_first, n, ranges, _, ref, at = unit
+        count = sum(k_count for _, k_count in ranges)
         low = lax.broadcasted_iota(jnp.int32, (n, PAIR), 1) < HEAD_SIZE
         cols = pair_cols(hp)
         q = Q[q_first:q_first + n, cols]
         zero = jnp.zeros_like(q)
         both = jnp.concatenate([jnp.where(low, q, zero), jnp.where(low, zero, q)], axis=0)
-        s = nt_dot(both, K[k_row:k_row + count, cols])
+        parts = [nt_dot(both, K[k_row:k_row + k_count, cols]) for k_row, k_count in ranges]
+        s = parts[0] if len(parts) == 1 else jnp.concatenate(parts, axis=1)
         dist = ref[at:at + n, :count]
         s = jnp.concatenate([
             jnp.where(dist <= window[2 * hp], s[:n], NEG),
@@ -216,8 +217,8 @@
         T[r0:r0 + 2 * n, :] = jnp.broadcast_to(top, (2 * n, PAIR))
 
     def values(unit, hp, S, T, first, last, r0=0):
-        q_first, n, k_row, segments, _, _ = unit
-        count = sum(k_count for _, k_count in segments)
+        q_first, n, ranges, _, _, _ = unit
+        count = sum(k_count for _, k_count in ranges)
         low = lax.broadcasted_iota(jnp.int32, (n, PAIR), 1) < HEAD_SIZE
         cols = pair_cols(hp)
         vcols = pl.ds(pl.multiple_of(hp * 2 * PAIR, 2 * PAIR), 2 * PAIR)
@@ -226,12 +227,17 @@
         if not first:
             old = jnp.concatenate([M[hp, 0, q_rows, :], M[hp, 1, q_rows, :]], axis=0)
             top = jnp.maximum(top, old)
-        step = min(PAIR, count)
-        p = jnp.concatenate([
-            jnp.exp2(S[r0:r0 + 2 * n, i:i + step] - top[:, :step]).astype(BF16)
-            for i in range(0, count, step)
-        ], axis=1)
-        added = nn_dot(p, VO[k_row:k_row + count, vcols])
+        added = None
+        column = 0
+        for k_row, k_count in ranges:
+            step = min(PAIR, k_count)
+            p = jnp.concatenate([
+                jnp.exp2(S[r0:r0 + 2 * n, i:i + step] - top[:, :step]).astype(BF16)
+                for i in range(column, column + k_count, step)
+            ], axis=1)
+            part = nn_dot(p, VO[k_row:k_row + k_count, vcols])
+            added = part if added is None else added + part
+            column += k_count
         acc = jnp.where(low, added[:n, :PAIR], added[n:, :PAIR])
         sums = jnp.where(low, added[:n, PAIR:], added[n:, PAIR:])
         if not first:
@@ -248,13 +254,7 @@
             L[q_rows, cols] = sums
 
     def attend(units, first, last):
-        if len(units) == 4:
-            batches = [
-                [(unit, 0, 2 * RC * b) for b, unit in enumerate(units[2 * i:2 * i + 2])]
-                for i in range(2)
-            ]
-            step = 1
-        elif units[0][1] == R:
+        if units[0][1] == R:
             batches = [[(units[0], 0, 0)], [(units[1], 0, 0)]]
             step = 1
         else:
@@ -279,29 +279,33 @@
             all_scores(batches[0], jnp.minimum(hp + step, pairs - step), S0, T0)
             all_values(batches[1], hp, S1, T1)
 
+    own = [(b * R, R, ((0, B),), ((0, B),), DIST, b * R) for b in range(2)]
+    near_out = [
+        (0, RC, ((B, B - RC),), ((-R, R), (B, RC)), DNO, 0),
+        (R + RC, RC, ((B + RC, B - RC),), ((-RC, RC), (B, R)), DNO, RC),
+    ]
+    near_segments = ((-R, R), (B, R))
+    mid = [
+        (RC, RC, ((B, B), (2 * B + RC, RC)), near_segments + ((-B + RC, RC),), DMID, 0),
+        (R, RC, ((B, B), (2 * B + R, RC)), near_segments + ((B + R, RC),), DMID, RC),
+    ]
+    far_out = [
+        (0, RC, ((2 * B, R),), ((-B, R),), DOUT, 0),
+        (R + RC, RC, ((2 * B + R, R),), ((B + R, R),), DOUT, RC),
+    ]
+
     own_load.wait()
+    loads[0].wait()
+    project([(own_rows, R)], True)
     sib_copy.wait_recv()
-    loads[0].wait()
-    project([(0, B)], True)
+    project([(pl.multiple_of(other * R, R), R)], True)
     halo_sent(0, 0)
     start_halo(1)
-    own = [(b * R, R, 0, ((0, B),), DIST, b * R) for b in range(2)]
     for unit in own:
         distances(unit)
     attend(own, True, False)
-
-    for k in range(2):
-        halo_arrived(0, k)
-    project([(B, B)], False)
-    near = [
-        (0, RC, B, ((-R, R), (B, RC)), DIST, 0),
-        (RC, RC, B, ((-R, R), (B, R)), DIST, RC),
-        (R, RC, B, ((-R, R), (B, R)), DIST, R),
-        (R + RC, RC, B + RC, ((-RC, RC), (B, R)), DIST, R + RC),
-    ]
-    for unit in near:
+    for unit in near_out + mid + far_out:
         distances(unit)
-    attend(near, False, False)
 
     n = members * CH
     row_i = lax.broadcasted_iota(jnp.int32, (n, members), 0)
@@ -315,17 +319,6 @@
     j2 = lax.broadcasted_iota(jnp.int32, (n, n), 1) & (CH - 1)
     KR[...] = jnp.where(i2 == j2, full_mix, 0.0).astype(BF16)
 
-    far_mid = [
-        (RC, RC, 2 * B + RC, ((-B + RC, RC),), DMID, 0),
-        (R, RC, 2 * B + R, ((B + R, RC),), DMID, RC),
-    ]
-    far_out = [
-        (0, RC, 2 * B, ((-B, R),), DOUT, 0),
-        (R + RC, RC, 2 * B + R, ((B + R, R),), DOUT, RC),
-    ]
-    for unit in far_mid + far_out:
-        distances(unit)
-
     def rows_of(group, core):
         return (RC + core * RC) if group == 0 else core * (R + RC)
 
@@ -424,9 +417,13 @@
 
     mid_rows = [(RC, R)]
     out_rows = [(0, RC), (R + RC, RC)]
+    for k in range(2):
+        halo_arrived(0, k)
+    project([(B, B)], False)
+    attend(near_out, False, False)
     halo_arrived(1, 0)
     project([(2 * B + RC, R)], False)
-    attend(far_mid, False, True)
+    attend(mid, False, True)
     loads[1].wait()
     loads[2].wait()
     finish_rows(0, mid_rows)
@@ -453,6 +450,10 @@
             spread_copy(group, j).wait_send()
         for j in range(1, groups):
             back_copy(group, j).wait_send()
+
+
+def put_kernel(hidden, mixed, wu, out):
+    out[...] = (hidden[...].astype(F32) + nn_dot(mixed[...], wu[...])).astype(BF16)
 
 
 def on_device(
@@ -487,10 +488,11 @@
             pltpu.VMEM((B, D), F32),
             pltpu.VMEM((B, D), F32),
             pltpu.VMEM((B, B), jnp.int32),
-            pltpu.VMEM((R, RC), jnp.int32),
+            pltpu.VMEM((R, B - RC), jnp.int32),
+            pltpu.VMEM((R, B + RC), jnp.int32),
             pltpu.VMEM((R, R), jnp.int32),
-            pltpu.VMEM((B, B), F32),
-            pltpu.VMEM((B, B), F32),
+            pltpu.VMEM((B, B + RC), F32),
+            pltpu.VMEM((B, B + RC), F32),
             pltpu.VMEM((B, PAIR), F32),
             pltpu.VMEM((B, PAIR), F32),
             pltpu.VMEM((B, D), BF16),
@@ -510,8 +512,21 @@
         ),
         name="layer",
     )(lengths, head_window, series_mix, history, input_proj, output_proj, mixer_down)
-    update = jnp.einsum("spc,cd->spd", mixed, mixer_up, preferred_element_type=F32)
-    return (hidden.astype(F32) + update).astype(BF16)
+    rows = S * R
+    block = rows // 4
+    layer_out = pl.pallas_call(
+        put_kernel,
+        grid=(4,),
+        out_shape=jax.ShapeDtypeStruct((rows, D), BF16),
+        in_specs=[
+            pl.BlockSpec((block, D), lambda i: (i, 0)),
+            pl.BlockSpec((block, C), lambda i: (i, 0)),
+            pl.BlockSpec((C, D), lambda i: (0, 0)),
+        ],
+        out_specs=pl.BlockSpec((block, D), lambda i: (i, 0)),
+        name="put",
+    )(hidden.reshape(rows, D), mixed.reshape(rows, C), mixer_up)
+    return layer_out.reshape(S, R, D)
 
 
 def solution(mesh):

time: 69.6 us -> 69.4 us (level)
  matrix products: 3.39 us -> 0 us
  Pallas kernels: 65.1 us -> 68.2 us
    pallas_call x0 -> x1, Pallas kernels: none -> 4.54 us  [on_device(): pl.pallas_call(put_kernel, grid=(4,), out_shape=jax.ShapeDtypeStruct((row...]
    dot_general x1 -> x0, matrix products: 3.39 us -> none  [on_device(): jnp.einsum('spc,cd->spd', mixed, mixer_up, preferred_element_type=F32)]
    pallas_call x1, Pallas kernels: 65.1 us -> 63.7 us  [on_device(): pl.pallas_call(functools.partial(layer_kernel, (chips, groups)), out_shap...]
where the time goes in v4:
time: 69.4 us; the launch traced here: 68.3 us
  Pallas kernels  68.2 us (98%)
    pallas_call x1, Pallas kernels, on_device(): pl.pallas_call(functools.partial(layer_kernel, (chips, groups)), out_shap...  63.7 us
    pallas_call x1, Pallas kernels, on_device(): pl.pallas_call(put_kernel, grid=(4,), out_shape=jax.ShapeDtypeStruct((row...  4.54 us

profile of v4, /device:TPU:9, one launch (start us, length us, event | category | flops | bytes accessed | tf_op | source)
XLA Modules:
  0.0 68.3 jit_solution(6975803841996202608)
XLA Ops:
  0.0 63.7 %layer.1 = (bf16[2,256,1024]{2,1,0:T(8,128)(2,1)}, bf16[2,256,512]{2,1,0:T(8,128)(2,1)}) custom-call(s32[2]{0:T(128)} %lengths.1, s32[16]{0:T(128)} %window.1, bf16[16,16]{1,0:T(8,128)(2,1)} %mix.1, bf16[2,256,1024]{2,1,0:T(8,128)(2,1)} %hist.1, bf16[1024,3072]{1,0:T(8,128)(2,1)} %wi_any.1, bf16[1024,1024]{1,0:T(8,128)(2,1)} %wo_any.1, bf16[1024,512]{1,0:T(8,128)(2,1)} %wd_any.1), custom_call_target="tpu_custom_call" | custom-call | tf_op jit(solution)/shard_map/layer/pallas_call | solution.py:475
  63.7 4.5 %put.1 = bf16[512,1024]{1,0:T(8,128)(2,1)} custom-call(bf16[512,1024]{1,0:T(8,128)(2,1)} %bitcast.3, bf16[512,512]{1,0:T(8,128)(2,1)} %bitcast.4, bf16[512,1024]{1,0:T(8,128)(2,1)} %wu.1), custom_call_target="tpu_custom_call" | custom-call | tf_op jit(solution)/shard_map/put/pallas_call | solution.py:517

commit v5 on v4

--- a/solution.py
+++ b/solution.py
@@ -254,7 +254,10 @@
             L[q_rows, cols] = sums
 
     def attend(units, first, last):
-        if units[0][1] == R:
+        if len(units) == 1:
+            batches = [[(units[0], 2 * i + b, 2 * RC * b) for b in range(2)] for i in range(2)]
+            step = 4
+        elif units[0][1] == R:
             batches = [[(units[0], 0, 0)], [(units[1], 0, 0)]]
             step = 1
         else:
@@ -297,14 +300,7 @@
     own_load.wait()
     loads[0].wait()
     project([(own_rows, R)], True)
-    sib_copy.wait_recv()
-    project([(pl.multiple_of(other * R, R), R)], True)
-    halo_sent(0, 0)
-    start_halo(1)
-    for unit in own:
-        distances(unit)
-    attend(own, True, False)
-    for unit in near_out + mid + far_out:
+    for unit in own + near_out + mid + far_out:
         distances(unit)
 
     n = members * CH
@@ -319,6 +315,12 @@
     j2 = lax.broadcasted_iota(jnp.int32, (n, n), 1) & (CH - 1)
     KR[...] = jnp.where(i2 == j2, full_mix, 0.0).astype(BF16)
 
+    sib_copy.wait_recv()
+    project([(pl.multiple_of(other * R, R), R)], True)
+    halo_sent(0, 0)
+    start_halo(1)
+    attend(own, True, False)
+
     def rows_of(group, core):
         return (RC + core * RC) if group == 0 else core * (R + RC)
 
@@ -386,7 +388,7 @@
             CB.at[group, pl.ds(2 * g, 2)], mix_out.at[:, pl.ds(row, CH), :], loc_sem.at[6 + group]
         )
 
-    def finish_rows(group, rows):
+    def finish_rows(group, rows, cores):
         @pl.loop(0, D // tile)
         def _(j):
             cols = pl.ds(pl.multiple_of(j * tile, tile), tile)
@@ -394,18 +396,29 @@
             update = nn_dot(stacked(ATT, rows), wo[:, cols])
             scatter(HID, rows, cols, (own_x.astype(F32) + update).astype(BF16))
 
-        hidden_copy(group).start()
-        hidden_keep(group).start()
+        if cores[-1] == 1:
+            hidden_copy(group).start()
+            hidden_keep(group).start()
 
         @pl.loop(0, C // tile)
         def _(j):
             cols = pl.ds(pl.multiple_of(j * tile, tile), tile)
             scatter(BR, rows, cols, nn_dot(stacked(HID, rows), wd[:, cols]).astype(BF16))
 
-        for j in range(1, members):
-            spread_copy(group, j).start()
-        row = pl.multiple_of(rows_of(group, c) + g * CH, CH)
-        RX[group, pl.ds(pl.multiple_of(mine * CH, CH), CH), :] = BR[pl.ds(row, CH), :]
+        for core in cores:
+            plus = lax.rem(c + core, 2)
+
+            @pl.when(plus == 0)
+            def _():
+                row = pl.multiple_of(rows_of(group, c) + g * CH, CH)
+                RX[group, pl.ds(pl.multiple_of(mine * CH, CH), CH), :] = BR[pl.ds(row, CH), :]
+
+            @pl.when(plus == 1)
+            def _():
+                spread_copy(group, 1).start()
+
+            for i in range(1, groups):
+                spread_copy(group, 2 * i + plus).start()
 
     def mix_rows(group):
         for j in range(1, members):
@@ -426,11 +439,12 @@
     attend(mid, False, True)
     loads[1].wait()
     loads[2].wait()
-    finish_rows(0, mid_rows)
+    finish_rows(0, mid_rows, (0, 1))
     halo_arrived(1, 1)
     project([(halo_row(1, 0, 1), RC), (halo_row(1, 1, 1), RC)], False)
-    attend(far_out, False, True)
-    finish_rows(1, out_rows)
+    for core in range(2):
+        attend(far_out[core:core + 1], False, True)
+        finish_rows(1, out_rows[core:core + 1], (core,))
     mix_rows(0)
     mix_rows(1)
     for group in range(2):
@@ -450,10 +464,6 @@
             spread_copy(group, j).wait_send()
         for j in range(1, groups):
             back_copy(group, j).wait_send()
-
-
-def put_kernel(hidden, mixed, wu, out):
-    out[...] = (hidden[...].astype(F32) + nn_dot(mixed[...], wu[...])).astype(BF16)
 
 
 def on_device(
@@ -512,21 +522,8 @@
         ),
         name="layer",
     )(lengths, head_window, series_mix, history, input_proj, output_proj, mixer_down)
-    rows = S * R
-    block = rows // 4
-    layer_out = pl.pallas_call(
-        put_kernel,
-        grid=(4,),
-        out_shape=jax.ShapeDtypeStruct((rows, D), BF16),
-        in_specs=[
-            pl.BlockSpec((block, D), lambda i: (i, 0)),
-            pl.BlockSpec((block, C), lambda i: (i, 0)),
-            pl.BlockSpec((C, D), lambda i: (0, 0)),
-        ],
-        out_specs=pl.BlockSpec((block, D), lambda i: (i, 0)),
-        name="put",
-    )(hidden.reshape(rows, D), mixed.reshape(rows, C), mixer_up)
-    return layer_out.reshape(S, R, D)
+    update = jnp.einsum("spc,cd->spd", mixed, mixer_up, preferred_element_type=F32)
+    return (hidden.astype(F32) + update).astype(BF16)
 
 
 def solution(mesh):

time: 69.4 us -> 67.6 us (0.974); the launches traced: 68.3 us -> 67.4 us
  Pallas kernels: 68.2 us -> 64 us
  matrix products: 0 us -> 3.39 us
    pallas_call x1 -> x0, Pallas kernels: 4.54 us -> none  [on_device(): pl.pallas_call(put_kernel, grid=(4,), out_shape=jax.ShapeDtypeStruct((row...]
    dot_general x0 -> x1, matrix products: none -> 3.39 us  [on_device(): jnp.einsum('spc,cd->spd', mixed, mixer_up, preferred_element_type=F32)]
where the time goes in v5:
time: 67.6 us; the launch traced here: 67.4 us
  Pallas kernels  64 us (95%)
  matrix products  3.39 us (5%)
    pallas_call x1, Pallas kernels, on_device(): pl.pallas_call(functools.partial(layer_kernel, (chips, groups)), out_shap...  64 us
    dot_general x1, matrix products, on_device(): jnp.einsum('spc,cd->spd', mixed, mixer_up, preferred_element_type=F32)  3.39 us

profile of v5, /device:TPU:9, one launch (start us, length us, event | category | flops | bytes accessed | tf_op | source)
XLA Modules:
  0.0 67.4 jit_solution(3252042397456040099)
XLA Ops:
  0.0 64.0 %layer.1 = (bf16[2,256,1024]{2,1,0:T(8,128)(2,1)}, bf16[2,256,512]{2,1,0:T(8,128)(2,1)}) custom-call(s32[2]{0:T(128)} %lengths.1, s32[16]{0:T(128)} %window.1, bf16[16,16]{1,0:T(8,128)(2,1)} %mix.1, bf16[2,256,1024]{2,1,0:T(8,128)(2,1)} %hist.1, bf16[1024,3072]{1,0:T(8,128)(2,1)} %wi_any.1, bf16[1024,1024]{1,0:T(8,128)(2,1)} %wo_any.1, bf16[1024,512]{1,0:T(8,128)(2,1)} %wd_any.1), custom_call_target="tpu_custom_call" | custom-call | tf_op jit(solution)/shard_map/layer/pallas_call | solution.py:485
  64.0 3.4 %add_convert_fusion = bf16[2,256,1024]{2,1,0:T(8,128)(2,1)} fusion(bf16[2,256,1024]{2,1,0:T(8,128)(2,1)} %get-tuple-element.7, bf16[2,256,512]{2,1,0:T(8,128)(2,1)} %get-tuple-element.8, bf16[512,1024]{1,0:T(8,128)(2,1)} %param.14), kind=kOutput, calls=%fused_computation | convolution fusion | flops 538443776 | bytes 3670016 | tf_op jit(solution)/shard_map/spc,cd->spd/dot_general | solution.py:525

commit v6 on v5

--- a/solution.py
+++ b/solution.py
@@ -213,8 +213,10 @@
             jnp.where(dist <= window[2 * hp + 1], s[n:], NEG),
         ], axis=0)
         S[r0:r0 + 2 * n, :count] = s
-        top = jnp.max(s, axis=1, keepdims=True)
-        T[r0:r0 + 2 * n, :] = jnp.broadcast_to(top, (2 * n, PAIR))
+        lanes = min(PAIR, count)
+        T[r0:r0 + 2 * n, :lanes] = functools.reduce(
+            jnp.maximum, [s[:, i:i + lanes] for i in range(0, count, lanes)]
+        )
 
     def values(unit, hp, S, T, first, last, r0=0):
         q_first, n, ranges, _, _, _ = unit
@@ -223,7 +225,9 @@
         cols = pair_cols(hp)
         vcols = pl.ds(pl.multiple_of(hp * 2 * PAIR, 2 * PAIR), 2 * PAIR)
         q_rows = slice(q_first, q_first + n)
-        top = T[r0:r0 + 2 * n, :]
+        lanes = min(PAIR, count)
+        top = jnp.max(T[r0:r0 + 2 * n, :lanes], axis=1, keepdims=True)
+        top = jnp.broadcast_to(top, (2 * n, PAIR))
         if not first:
             old = jnp.concatenate([M[hp, 0, q_rows, :], M[hp, 1, q_rows, :]], axis=0)
             top = jnp.maximum(top, old)
@@ -389,9 +393,11 @@
         )
 
     def finish_rows(group, rows, cores):
-        @pl.loop(0, D // tile)
+        wide = min(2 * tile, C)
+
+        @pl.loop(0, D // wide)
         def _(j):
-            cols = pl.ds(pl.multiple_of(j * tile, tile), tile)
+            cols = pl.ds(pl.multiple_of(j * wide, wide), wide)
             own_x = stacked(X, rows, cols)
             update = nn_dot(stacked(ATT, rows), wo[:, cols])
             scatter(HID, rows, cols, (own_x.astype(F32) + update).astype(BF16))
@@ -400,9 +406,9 @@
             hidden_copy(group).start()
             hidden_keep(group).start()
 
-        @pl.loop(0, C // tile)
+        @pl.loop(0, C // wide)
         def _(j):
-            cols = pl.ds(pl.multiple_of(j * tile, tile), tile)
+            cols = pl.ds(pl.multiple_of(j * wide, wide), wide)
             scatter(BR, rows, cols, nn_dot(stacked(HID, rows), wd[:, cols]).astype(BF16))
 
         for core in cores:

time: 67.6 us -> 66 us (0.976)
  Pallas kernels: 64 us -> 62.4 us
    pallas_call x1, Pallas kernels: 64 us -> 62.4 us  [on_device(): pl.pallas_call(functools.partial(layer_kernel, (chips, groups)), out_shap...]
where the time goes in v6:
time: 66 us; the launch traced here: 65.8 us
  Pallas kernels  62.4 us (95%)
  matrix products  3.39 us (5%)
    pallas_call x1, Pallas kernels, on_device(): pl.pallas_call(functools.partial(layer_kernel, (chips, groups)), out_shap...  62.4 us
    dot_general x1, matrix products, on_device(): jnp.einsum('spc,cd->spd', mixed, mixer_up, preferred_element_type=F32)  3.39 us

profile of v6, /device:TPU:9, one launch (start us, length us, event | category | flops | bytes accessed | tf_op | source)
XLA Modules:
  0.0 65.8 jit_solution(10162136283934961040)
XLA Ops:
  0.0 62.4 %layer.1 = (bf16[2,256,1024]{2,1,0:T(8,128)(2,1)}, bf16[2,256,512]{2,1,0:T(8,128)(2,1)}) custom-call(s32[2]{0:T(128)} %lengths.1, s32[16]{0:T(128)} %window.1, bf16[16,16]{1,0:T(8,128)(2,1)} %mix.1, bf16[2,256,1024]{2,1,0:T(8,128)(2,1)} %hist.1, bf16[1024,3072]{1,0:T(8,128)(2,1)} %wi_any.1, bf16[1024,1024]{1,0:T(8,128)(2,1)} %wo_any.1, bf16[1024,512]{1,0:T(8,128)(2,1)} %wd_any.1), custom_call_target="tpu_custom_call" | custom-call | tf_op jit(solution)/shard_map/layer/pallas_call | solution.py:491
  62.4 3.4 %add_convert_fusion = bf16[2,256,1024]{2,1,0:T(8,128)(2,1)} fusion(bf16[2,256,1024]{2,1,0:T(8,128)(2,1)} %get-tuple-element.7, bf16[2,256,512]{2,1,0:T(8,128)(2,1)} %get-tuple-element.8, bf16[512,1024]{1,0:T(8,128)(2,1)} %param.14), kind=kOutput, calls=%fused_computation | convolution fusion | flops 538443776 | bytes 3670016 | tf_op jit(solution)/shard_map/spc,cd->spd/dot_general | solution.py:531

commit v7 on v6

--- a/solution.py
+++ b/solution.py
@@ -257,7 +257,7 @@
             ACC[q_rows, cols] = acc
             L[q_rows, cols] = sums
 
-    def attend(units, first, last):
+    def attend(units, first, last, start=0, stop=None):
         if len(units) == 1:
             batches = [[(units[0], 2 * i + b, 2 * RC * b) for b in range(2)] for i in range(2)]
             step = 4
@@ -276,9 +276,11 @@
             for unit, plus, r0 in batch:
                 values(unit, hp + plus, S, T, first, last, r0)
 
-        all_scores(batches[0], 0, S0, T0)
-
-        @pl.loop(0, pairs // step)
+        if start == 0:
+            all_scores(batches[0], 0, S0, T0)
+        stop = pairs if stop is None else stop
+
+        @pl.loop(start // step, stop // step)
         def _(i):
             hp = i * step
             all_scores(batches[1], hp, S1, T1)
@@ -321,9 +323,11 @@
 
     sib_copy.wait_recv()
     project([(pl.multiple_of(other * R, R), R)], True)
+    part = pairs // 4
+    attend(own, True, False, 0, part)
     halo_sent(0, 0)
     start_halo(1)
-    attend(own, True, False)
+    attend(own, True, False, part)
 
     def rows_of(group, core):
         return (RC + core * RC) if group == 0 else core * (R + RC)

time: 66 us -> 65.1 us (0.986)
  Pallas kernels: 62.4 us -> 61.6 us
    pallas_call x1, Pallas kernels: 62.4 us -> 61.6 us  [on_device(): pl.pallas_call(functools.partial(layer_kernel, (chips, groups)), out_shap...]
where the time goes in v7:
time: 65.1 us; the launch traced here: 65 us
  Pallas kernels  61.6 us (95%)
  matrix products  3.39 us (5%)
    pallas_call x1, Pallas kernels, on_device(): pl.pallas_call(functools.partial(layer_kernel, (chips, groups)), out_shap...  61.6 us
    dot_general x1, matrix products, on_device(): jnp.einsum('spc,cd->spd', mixed, mixer_up, preferred_element_type=F32)  3.39 us

profile of v7, /device:TPU:9, one launch (start us, length us, event | category | flops | bytes accessed | tf_op | source)
XLA Modules:
  0.0 65.0 jit_solution(3132762271840426673)
XLA Ops:
  0.0 61.6 %layer.1 = (bf16[2,256,1024]{2,1,0:T(8,128)(2,1)}, bf16[2,256,512]{2,1,0:T(8,128)(2,1)}) custom-call(s32[2]{0:T(128)} %lengths.1, s32[16]{0:T(128)} %window.1, bf16[16,16]{1,0:T(8,128)(2,1)} %mix.1, bf16[2,256,1024]{2,1,0:T(8,128)(2,1)} %hist.1, bf16[1024,3072]{1,0:T(8,128)(2,1)} %wi_any.1, bf16[1024,1024]{1,0:T(8,128)(2,1)} %wo_any.1, bf16[1024,512]{1,0:T(8,128)(2,1)} %wd_any.1), custom_call_target="tpu_custom_call" | custom-call | tf_op jit(solution)/shard_map/layer/pallas_call | solution.py:495
  61.6 3.4 %add_convert_fusion = bf16[2,256,1024]{2,1,0:T(8,128)(2,1)} fusion(bf16[2,256,1024]{2,1,0:T(8,128)(2,1)} %get-tuple-element.7, bf16[2,256,512]{2,1,0:T(8,128)(2,1)} %get-tuple-element.8, bf16[512,1024]{1,0:T(8,128)(2,1)} %param.14), kind=kOutput, calls=%fused_computation | convolution fusion | flops 538443776 | bytes 3670016 | tf_op jit(solution)/shard_map/spc,cd->spd/dot_general | solution.py:535
